TPU v7x, 256 devices: a whole 4x4x8 slice. The times are simulated.
256 devices in a mesh: chan: 64 (over y, z, core), slot: 4 (over x).
Axes of the slice: x: 4, y: 4, z: 8, core: 2. Of those that a mesh axis runs over, the one named last changes fastest.
Arguments:
- visibility: float32 [2, 2, 256, 4, 3844], P(None, None, 'chan', 'slot'), parts along dimension 3, may hold values from -6 to 6
- coherency: bfloat16 [2, 2, 16, 256, 4, 3844], P(None, None, None, 'chan', 'slot'), parts along dimension 4, may hold values from -2 to 2
- jones_start: float32 [2, 2, 64, 256, 62], P(None, None, 'slot', 'chan'), parts along dimension 2, may hold values from -4 to 4
- duals_start: float32 [2, 2, 64, 256, 62], P(None, None, 'slot', 'chan'), parts along dimension 2, may hold values from -2 to 2
Outputs:
- jones_final: float32 [2, 2, 64, 256, 62], P(None, None, 'slot', 'chan'), parts along dimension 2
- consensus: float32 [2, 2, 64, 256, 62], P(None, None, 'slot', 'chan'), parts along dimension 2
- duals_final: float32 [2, 2, 64, 256, 62], P(None, None, 'slot', 'chan'), parts along dimension 2
- norms: float32 [8, 2], P('slot'), parts along dimension 0
There are 4 independent parts, one for each index of `slot`. A program takes and returns all parts, laid end to end along the dimension named above; each array names one. Nothing has to cross between parts.
All inputs are finite; a program needn't handle non-finite values.
Results may differ from a plain program's by a relative error of at most 0.0003.
Values sent between devices are 32-bit elements; how exact they have to be, the bound alone decides.
A program may use at most 128 MiB of HBM per device.

v0:
```python
import jax
import jax.numpy as jnp
from jax import lax
from jax.sharding import PartitionSpec as P

ITERS = 2


penalty = 8.0
kernel_taps = (0.04, 0.06, 0.1, 0.15, 0.3, 0.15, 0.1, 0.06, 0.04)


def padded_2(block, sides, width):
    for axis, dim in sides:
        count = lax.axis_size(axis)
        forward = [(i, i + 1) for i in range(count - 1)]
        backward = [(target, source) for source, target in forward]
        low = lax.ppermute(
            lax.slice_in_dim(block, block.shape[dim] - width, None, axis=dim), axis, forward
        )
        high = lax.ppermute(lax.slice_in_dim(block, 0, width, axis=dim), axis, backward)
        block = jnp.concatenate([low, block, high], axis=dim)
    return block


def sent_to_all(x, axis):
    copies = jnp.broadcast_to(x, (lax.axis_size(axis), *x.shape))
    return lax.all_to_all(copies, axis, split_axis=0, concat_axis=0, tiled=True)


def taken_together(x, axis):
    everything = sent_to_all(x, axis)
    return jnp.sum(everything, axis=0)


def jones_update(visibility, coherency, jones_now, target):
    width = jones_now.shape[-1]
    grid_shape = coherency.shape[1:5] + (width, width)
    sky_real = coherency[0].astype(jnp.float32).reshape(grid_shape)
    sky_imag = coherency[1].astype(jnp.float32).reshape(grid_shape)
    vis_shape = visibility.shape[1:4] + (width, width)
    data_real = visibility[0].reshape(vis_shape)[:, None]
    data_imag = visibility[1].reshape(vis_shape)[:, None]
    left_real = jones_now[0][:, :, :, None, :, None]
    left_imag = jones_now[1][:, :, :, None, :, None]
    right_real = jones_now[0][:, :, :, None, None, :]
    right_imag = jones_now[1][:, :, :, None, None, :]
    crossed = 1.0 - jnp.eye(width, dtype=jnp.float32)
    half_real = left_real * sky_real - left_imag * sky_imag
    half_imag = left_real * sky_imag + left_imag * sky_real
    model_real = half_real * right_real + half_imag * right_imag
    model_imag = half_imag * right_real - half_real * right_imag
    rest_real = (data_real - jnp.sum(model_real, axis=1, keepdims=True) + model_real) * crossed
    rest_imag = (data_imag - jnp.sum(model_imag, axis=1, keepdims=True) + model_imag) * crossed
    weight_real = sky_real * right_real + sky_imag * right_imag
    weight_imag = sky_real * right_imag - sky_imag * right_real
    upper_real = jnp.sum(rest_real * weight_real - rest_imag * weight_imag, axis=(3, 5))
    upper_imag = jnp.sum(rest_real * weight_imag + rest_imag * weight_real, axis=(3, 5))
    lower = (
        jnp.sum(
            crossed
            * (sky_real * sky_real + sky_imag * sky_imag)
            * (right_real * right_real + right_imag * right_imag),
            axis=(3, 5),
        )
        + penalty
    )
    return jnp.stack(
        [(upper_real + penalty * target[0]) / lower, (upper_imag + penalty * target[1]) / lower]
    )


def smooth(padded, channels):
    total = kernel_taps[0] * padded[:, :, :, 0:channels]
    for offset in range(1, 9):
        total = total + kernel_taps[offset] * padded[:, :, :, offset : offset + channels]
    return total


def local(visibility, coherency, jones_start, duals_start):
    channels = jones_start.shape[3]
    entries = jones_start.size * lax.axis_size("chan")
    jones_now = jones_start
    consensus = jones_start
    duals_now = duals_start
    partials = []
    for iteration in range(ITERS):
        jones_now = jones_update(visibility, coherency, jones_now, consensus - duals_now)
        padded = padded_2(jones_now + duals_now, (("chan", 3),), 4)
        fresh = smooth(padded, channels)
        duals_now = duals_now + jones_now - fresh
        primal_gap = jones_now - fresh
        moved = fresh - consensus
        pieces = (jnp.sum(primal_gap * primal_gap), penalty * penalty * jnp.sum(moved * moved))
        partials.append(jnp.stack([pieces[0], pieces[1]]))
        consensus = fresh
    norms = taken_together(jnp.stack(partials), "chan") / entries
    return (jones_now, consensus, duals_now, norms)


def solution(mesh):
    placed = (
        P(None, None, "chan", "slot", None),
        P(None, None, None, "chan", "slot", None),
        P(None, None, "slot", "chan", None),
        P(None, None, "slot", "chan", None),
    )
    return jax.shard_map(
        local,
        mesh=mesh,
        in_specs=placed,
        out_specs=(
            P(None, None, "slot", "chan", None),
            P(None, None, "slot", "chan", None),
            P(None, None, "slot", "chan", None),
            P("slot", None),
        ),
        check_vma=False,
    )
```

profile of v0, /device:TPU:1, one launch (start us, length us, event | category | flops | bytes accessed | tf_op | source)
XLA Modules:
  0.0 159.5 jit_solution(7662246619976627062)
XLA Ops:
  3.1 2.5 %mul.1257 = f32[2,16,4,62,62]{4,3,1,2,0:T(8,128)} broadcast(f32[2,16,4,62]{3,1,2,0:T(8,128)S(1)} %copy.64), dimensions={0,1,2,3} | broadcast | bytes 1999872 | tf_op jit(solution)/shard_map/mul | solution.py:49
  5.6 5.0 %mul.1258 = f32[1,2,16,4,1,3844]{5,2,3,1,4,0:T(8,128)} reshape(f32[2,16,4,62,62]{4,3,1,2,0:T(8,128)} %mul.1257) | data formatting | bytes 3936256 | tf_op jit(solution)/shard_map/mul | solution.py:49
  10.6 2.5 %mul.1261 = f32[2,16,4,62,62]{4,3,1,2,0:T(8,128)} broadcast(f32[2,16,4,62]{3,1,2,0:T(8,128)S(1)} %copy.66), dimensions={0,1,2,3} | broadcast | bytes 1999872 | tf_op jit(solution)/shard_map/mul | solution.py:49
  13.1 5.0 %mul.1262 = f32[1,2,16,4,1,3844]{5,2,3,1,4,0:T(8,128)} reshape(f32[2,16,4,62,62]{4,3,1,2,0:T(8,128)} %mul.1261) | data formatting | bytes 3936256 | tf_op jit(solution)/shard_map/mul | solution.py:49
  20.3 5.0 %mul.1265 = f32[1,2,16,4,1,3844]{5,2,3,1,4,0:T(8,128)} reshape(f32[2,16,4,62,62]{4,3,1,2,0:T(8,128)} %mul.1264) | data formatting | bytes 3936256 | tf_op jit(solution)/shard_map/mul | solution.py:51
  27.5 5.0 %mul.1270 = f32[1,2,16,4,1,3844]{5,2,3,1,4,0:T(8,128)} reshape(f32[2,16,4,62,62]{4,3,1,2,0:T(8,128)} %mul.1269) | data formatting | bytes 3936256 | tf_op jit(solution)/shard_map/mul | solution.py:51
  32.5 2.4 %fusion.49 = (bf16[1,2,16,4,1,3844]{5,3,4,2,1,0:T(4,128)(2,1)S(1)}, bf16[1,2,16,4,1,3844]{5,3,4,2,1,0:T(4,128)(2,1)S(1)}) fusion(bf16[2,2,16,4,1,3844]{5,3,4,2,1,0:T(4,128)(2,1)} %param.5), kind=kLoop, calls=%fused_computation.123 | loop fusion | bytes 3936256 | tf_op jit(solution)/shard_map/slice | solution.py:39
  34.9 2.3 %copy_convert_fusion = (f32[1,2,16,4,1,3844]{5,2,3,1,4,0:T(8,128)}, f32[1,2,16,4,1,3844]{5,2,3,1,4,0:T(8,128)}) fusion(bf16[1,2,16,4,1,3844]{5,3,4,2,1,0:T(4,128)(2,1)S(1)} %get-tuple-element.40, bf16[1,2,16,4,1,3844]{5,3,4,2,1,0:T(4,128)(2,1)S(1)} %get-tuple-element.39), kind=kLoop, calls=%fused_computation.27 | loop fusion | flops 984064 | bytes 5904384 | tf_op jit(solution)/shard_map/convert_element_type | solution.py:40
  41.0 8.4 %reshape.965 = f32[2,16,4,1,62,62]{5,4,1,2,0,3:T(8,128)} reshape(f32[1,2,16,4,1,3844]{5,2,3,1,4,0:T(8,128)} %get-tuple-element.49) | data formatting | bytes 3936256 | tf_op jit(solution)/shard_map/convert_element_type | solution.py:39
  49.4 8.2 %reshape.966 = f32[2,16,4,1,62,62]{5,4,1,2,0,3:T(8,128)} reshape(f32[1,2,16,4,1,3844]{5,2,3,1,4,0:T(8,128)} %get-tuple-element.48) | data formatting | bytes 3936256 | tf_op jit(solution)/shard_map/convert_element_type | solution.py:40
  58.5 10.0 %subtract_reduce_fusion.1 = (f32[2,16,4,62]{3,1,2,0:T(8,128)S(1)}, f32[2,16,4,62]{3,1,2,0:T(8,128)S(1)}, f32[2,16,4,62]{3,1,2,0:T(8,128)S(1)}) fusion(f32[2,16,4,1,62,62]{5,4,1,2,0,3:T(8,128)} %reshape.966, f32[2,16,4,62]{3,1,2,0:T(8,128)S(1)} %copy.66, f32[2,16,4,1,62,62]{5,4,1,2,0,3:T(8,128)} %reshape.965, f32[2,16,4,62]{3,1,2,0:T(8,128)S(1)} %copy.64, ...), kind=kLoop, calls=%fused_computation.12 | loop fusion | flops 17689344 | bytes 4388112 | tf_op jit(solution)/shard_map/reduce_sum | solution.py:57
  68.6 4.9 %collective-permute-start = (f32[2,2,16,4,62]{4,2,3,1,0:T(8,128)S(1)}, f32[2,2,16,4,62]{4,2,3,1,0:T(8,128)}, u32[]{:S(2)}, u32[]{:S(2)}) collective-permute-start(f32[2,2,16,4,62]{4,2,3,1,0:T(8,128)S(1)} %copy_add_fusion), channel_id=1, source_target_pairs={{0,4},{4,8},{8,12},{12,16},{16,20},{20,24},{24,28},{28,32},{32,36}... | collective-permute-start | bytes 190472 | tf_op jit(solution)/shard_map/ppermute | solution.py:18
  75.7 2.6 %mul.1304 = f32[2,16,4,62,62]{4,3,1,2,0:T(8,128)} broadcast(f32[2,16,4,62]{3,1,2,0:T(8,128)S(1)} %get-tuple-element.34), dimensions={0,1,2,3} | broadcast | bytes 1999872 | tf_op jit(solution)/shard_map/mul | solution.py:49
  78.3 5.0 %mul.1305 = f32[1,2,16,4,1,3844]{5,2,3,1,4,0:T(8,128)} reshape(f32[2,16,4,62,62]{4,3,1,2,0:T(8,128)} %mul.1304) | data formatting | bytes 3936256 | tf_op jit(solution)/shard_map/mul | solution.py:49
  83.3 2.6 %mul.1311 = f32[2,16,4,62,62]{4,3,1,2,0:T(8,128)} broadcast(f32[2,16,4,62]{3,1,2,0:T(8,128)S(1)} %get-tuple-element.35), dimensions={0,1,2,3} | broadcast | bytes 1999872 | tf_op jit(solution)/shard_map/mul | solution.py:49
  85.8 5.0 %mul.1312 = f32[1,2,16,4,1,3844]{5,2,3,1,4,0:T(8,128)} reshape(f32[2,16,4,62,62]{4,3,1,2,0:T(8,128)} %mul.1311) | data formatting | bytes 3936256 | tf_op jit(solution)/shard_map/mul | solution.py:49
  93.1 5.0 %mul.1315 = f32[1,2,16,4,1,3844]{5,2,3,1,4,0:T(8,128)} reshape(f32[2,16,4,62,62]{4,3,1,2,0:T(8,128)} %mul.1314) | data formatting | bytes 3936256 | tf_op jit(solution)/shard_map/mul | solution.py:51
  100.3 5.0 %mul.1320 = f32[1,2,16,4,1,3844]{5,2,3,1,4,0:T(8,128)} reshape(f32[2,16,4,62,62]{4,3,1,2,0:T(8,128)} %mul.1319) | data formatting | bytes 3936256 | tf_op jit(solution)/shard_map/mul | solution.py:51
  105.3 4.9 %subtract_reduce_fusion.2 = (f32[2,4,3844]{2,1,0:T(4,128)S(1)}, f32[2,4,3844]{2,1,0:T(4,128)S(1)}) fusion(f32[1,2,16,4,1,3844]{5,2,3,1,4,0:T(8,128)} %mul.1320, f32[1,2,16,4,1,3844]{5,2,3,1,4,0:T(8,128)} %mul.1315, f32[1,2,16,4,1,3844]{5,2,3,1,4,0:T(8,128)} %mul.1312, bf16[1,2,16,4,1,3844]{5,3,4,2,1,0:T(4,128)(2,1)S(1)} %get-tuple-element.40, ...), kind=kLoop, calls=%fused_computation.19 | loop fusion | flops 7811008 | bytes 10086656 | tf_op jit(solution)/shard_map/reduce_sum | solution.py:54
  111.0 10.0 %subtract_reduce_fusion = (f32[2,16,4,62]{3,1,2,0:T(8,128)S(1)}, f32[2,16,4,62]{3,1,2,0:T(8,128)S(1)}, f32[2,16,4,62]{3,1,2,0:T(8,128)S(1)}) fusion(f32[2,16,4,1,62,62]{5,4,1,2,0,3:T(8,128)} %reshape.966, f32[2,16,4,62]{3,1,2,0:T(8,128)S(1)} %get-tuple-element.35, f32[2,16,4,1,62,62]{5,4,1,2,0,3:T(8,128)} %reshape.965, ...), kind=kLoop, calls=%fused_computation.2 | loop fusion | flops 17689344 | bytes 4388112 | tf_op jit(solution)/shard_map/reduce_sum | solution.py:57
  122.3 3.4 %collective-permute-start.2 = (f32[2,2,16,4,62]{4,2,3,1,0:T(8,128)S(1)}, f32[2,2,16,4,62]{4,2,3,1,0:T(8,128)S(1)}, u32[]{:S(2)}, u32[]{:S(2)}) collective-permute-start(f32[2,2,16,4,62]{4,2,3,1,0:T(8,128)S(1)} %fusion.43), channel_id=1, source_target_pairs={{0,4},{4,8},{8,12},{12,16},{16,20},{20,24},{24,28},{28,32},{32,36}... | collective-permute-start | bytes 190472 | tf_op jit(solution)/shard_map/ppermute | solution.py:18
  127.7 4.3 %collective-permute-done.3 = f32[2,2,16,4,62]{4,2,3,1,0:T(8,128)S(1)} collective-permute-done((f32[2,2,16,4,62]{4,2,3,1,0:T(8,128)S(1)}, f32[2,2,16,4,62]{4,2,3,1,0:T(8,128)S(1)}, u32[]{:S(2)}, u32[]{:S(2)}) %collective-permute-start.3) | collective-permute-done | bytes 63520 | tf_op jit(solution)/shard_map/ppermute | solution.py:21
  136.3 12.8 %all-to-all-start = ((f32[64,2,2]{2,1,0:T(2,128)}), f32[64,2,2]{2,1,0:T(2,128)S(1)}, u32[]{:S(2)}, u32[]{:S(2)}) async-start(f32[64,2,2]{2,1,0:T(2,128)} %broadcast_in_dim.25), calls=%async_computation | async-start | bytes 131072 | tf_op jit(solution)/shard_map/all_to_all | solution.py:28
  151.3 7.6 %all-to-all-done = f32[64,2,2]{2,1,0:T(2,128)S(1)} async-done(((f32[64,2,2]{2,1,0:T(2,128)}), f32[64,2,2]{2,1,0:T(2,128)S(1)}, u32[]{:S(2)}, u32[]{:S(2)}) %all-to-all-start) | async-done | bytes 1056 | tf_op jit(solution)/shard_map/all_to_all | solution.py:28
  (59 shorter events, 27.8 us)
Async XLA Ops:
  32.5 4.7 %copy-start = (f32[1,2,16,4,1,3844]{5,2,3,1,4,0:T(8,128)S(1)}, f32[1,2,16,4,1,3844]{5,2,3,1,4,0:T(8,128)}, u32[]{:S(2)}) copy-start(f32[1,2,16,4,1,3844]{5,2,3,1,4,0:T(8,128)} %mul.1258) | copy-start | bytes 5904388
  32.5 4.7 %copy-start.1 = (f32[1,2,16,4,1,3844]{5,2,3,1,4,0:T(8,128)S(1)}, f32[1,2,16,4,1,3844]{5,2,3,1,4,0:T(8,128)}, u32[]{:S(2)}) copy-start(f32[1,2,16,4,1,3844]{5,2,3,1,4,0:T(8,128)} %mul.1262) | copy-start | bytes 5904388
  32.5 4.7 %copy-start.2 = (f32[1,2,16,4,1,3844]{5,2,3,1,4,0:T(8,128)S(1)}, f32[1,2,16,4,1,3844]{5,2,3,1,4,0:T(8,128)}, u32[]{:S(2)}) copy-start(f32[1,2,16,4,1,3844]{5,2,3,1,4,0:T(8,128)} %mul.1265) | copy-start | bytes 5904388
  32.5 4.7 %copy-start.3 = (f32[1,2,16,4,1,3844]{5,2,3,1,4,0:T(8,128)S(1)}, f32[1,2,16,4,1,3844]{5,2,3,1,4,0:T(8,128)}, u32[]{:S(2)}) copy-start(f32[1,2,16,4,1,3844]{5,2,3,1,4,0:T(8,128)} %mul.1270) | copy-start | bytes 5904388
  37.2 2.0 %copy-start.6 = (f32[2,2,4,1,3844]{4,3,2,1,0:T(1,128)S(1)}, f32[2,2,4,1,3844]{4,3,2,1,0:T(1,128)}, u32[]{:S(2)}) copy-start(f32[2,2,4,1,3844]{4,3,2,1,0:T(1,128)} %param.4) | copy-start | bytes 738052
  49.3 9.1 %copy-start.4 = (f32[2,2,16,4,62]{4,3,2,1,0:T(4,128)S(1)}, f32[2,2,16,4,62]{4,3,2,1,0:T(4,128)}, u32[]{:S(2)}) copy-start(f32[2,2,16,4,62]{4,3,2,1,0:T(4,128)} %param.6) | copy-start | bytes 190468
  49.4 9.1 %copy-start.5 = (f32[2,2,16,4,62]{4,3,2,1,0:T(4,128)S(1)}, f32[2,2,16,4,62]{4,3,2,1,0:T(4,128)}, u32[]{:S(2)}) copy-start(f32[2,2,16,4,62]{4,3,2,1,0:T(4,128)} %param.7) | copy-start | bytes 190468
  68.6 52.4 %collective-permute-start = (f32[2,2,16,4,62]{4,2,3,1,0:T(8,128)S(1)}, f32[2,2,16,4,62]{4,2,3,1,0:T(8,128)}, u32[]{:S(2)}, u32[]{:S(2)}) collective-permute-start(f32[2,2,16,4,62]{4,2,3,1,0:T(8,128)S(1)} %copy_add_fusion), channel_id=1, source_target_pairs={{0,4},{4,8},{8,12},{12,16},{16,20},{20,24},{24,28},{28,32},{32,36}... | collective-permute-start | bytes 190472 | tf_op jit(solution)/shard_map/ppermute | solution.py:18
  73.5 47.5 %collective-permute-start.1 = (f32[2,2,16,4,62]{4,2,3,1,0:T(8,128)S(1)}, f32[2,2,16,4,62]{4,2,3,1,0:T(8,128)}, u32[]{:S(2)}, u32[]{:S(2)}) collective-permute-start(f32[2,2,16,4,62]{4,2,3,1,0:T(8,128)S(1)} %copy_add_fusion), channel_id=1, source_target_pairs={{4,0},{8,4},{12,8},{16,12},{20,16},{24,20},{28,24},{32,28},{36,32}... | collective-permute-start | bytes 190472 | tf_op jit(solution)/shard_map/ppermute | solution.py:21
  122.3 5.4 %collective-permute-start.2 = (f32[2,2,16,4,62]{4,2,3,1,0:T(8,128)S(1)}, f32[2,2,16,4,62]{4,2,3,1,0:T(8,128)S(1)}, u32[]{:S(2)}, u32[]{:S(2)}) collective-permute-start(f32[2,2,16,4,62]{4,2,3,1,0:T(8,128)S(1)} %fusion.43), channel_id=1, source_target_pairs={{0,4},{4,8},{8,12},{12,16},{16,20},{20,24},{24,28},{28,32},{32,36}... | collective-permute-start | bytes 190472 | tf_op jit(solution)/shard_map/ppermute | solution.py:18
  125.8 6.3 %collective-permute-start.3 = (f32[2,2,16,4,62]{4,2,3,1,0:T(8,128)S(1)}, f32[2,2,16,4,62]{4,2,3,1,0:T(8,128)S(1)}, u32[]{:S(2)}, u32[]{:S(2)}) collective-permute-start(f32[2,2,16,4,62]{4,2,3,1,0:T(8,128)S(1)} %fusion.43), channel_id=1, source_target_pairs={{4,0},{8,4},{12,8},{16,12},{20,16},{24,20},{28,24},{32,28},{36,32}... | collective-permute-start | bytes 190472 | tf_op jit(solution)/shard_map/ppermute | solution.py:21
  136.3 22.6 %all-to-all-start = ((f32[64,2,2]{2,1,0:T(2,128)}), f32[64,2,2]{2,1,0:T(2,128)S(1)}, u32[]{:S(2)}, u32[]{:S(2)}) async-start(f32[64,2,2]{2,1,0:T(2,128)} %broadcast_in_dim.25), calls=%async_computation | async-start | bytes 131072 | tf_op jit(solution)/shard_map/all_to_all | solution.py:28
where the time goes:
time: 161 us; the launch traced here: 160 us
  local copies, waits for them, and re-layouts  85.3 us (53%)
  other arithmetic  34.8 us (22%)
  starting transfers between devices  25.2 us (16%)
  waiting for transfers between devices  12 us (7%)
  between operations  2.22 us (1%)
    mul x11, local copies, waits for them, and re-layouts, jones_update(): half_real = left_real * sky_real - left_imag * sky_imag  31.1 us
    mul x8, local copies, waits for them, and re-layouts, jones_update(): model_real = half_real * right_real + half_imag * right_imag  28.8 us
    reduce_sum x2, other arithmetic, jones_update(): jnp.sum(rest_real * weight_real - rest_imag * weight_imag, axis=(3, 5))  19.9 us
    all_to_all x1, starting transfers between devices, sent_to_all(): return lax.all_to_all(copies, axis, split_axis=0, concat_axis=0, tiled=True)  12.8 us
    convert_element_type x1, local copies, waits for them, and re-layouts, jones_update(): sky_real = coherency[0].astype(jnp.float32).reshape(grid_shape)  8.38 us
    ppermute x2, starting transfers between devices, padded_2(): lax.ppermute(lax.slice_in_dim(block, block.shape[dim] - width, None, axis...  8.37 us
    convert_element_type x1, local copies, waits for them, and re-layouts, jones_update(): sky_imag = coherency[1].astype(jnp.float32).reshape(grid_shape)  8.23 us
    all_to_all x1, waiting for transfers between devices, sent_to_all(): return lax.all_to_all(copies, axis, split_axis=0, concat_axis=0, tiled=True)  7.62 us
  transfers between devices with their start and end apart: 5, of which 2 were waited for; matrix products, arithmetic and copies ran while one was open for 30% of the time, Pallas kernels for 0%

commit v1 on v0

v1 whole, which is shorter than its diff:
```python
import functools

import jax
import jax.numpy as jnp
from jax import lax
from jax.experimental import pallas as pl
from jax.experimental.pallas import tpu as pltpu
from jax.sharding import PartitionSpec as P

STATIONS = 62
SIDE = 64
CHANS = 4
PAIRS = STATIONS * STATIONS
LANES = 128
FULL = PAIRS // LANES
TILES = FULL + 1
FLAT = STATIONS * SIDE + 2 * SIDE
BLOCK = 4
BLOCKS = SIDE // BLOCK
ROWS = BLOCK * SIDE

penalty = 8.0
kernel_taps = (0.04, 0.06, 0.1, 0.15, 0.3, 0.15, 0.1, 0.06, 0.04)
F32 = jnp.float32
BF16 = jnp.bfloat16


def to_chan(index):
    return {"chan": index}


def shifted(x, by):
    return x if by == 0 else pltpu.roll(x, (-by) % LANES, axis=1)


def smooth_own(own, channel):
    total = None
    for o in range(-3, 4):
        weight = jnp.where((channel + o >= 0) & (channel + o < CHANS), kernel_taps[o + 4], 0.0)
        term = shifted(own, o) * weight
        total = term if total is None else total + term
    return total


def smooth_sides(low, high, channel):
    total = None
    for o in range(1, 5):
        weight = jnp.where(channel - o < 0, kernel_taps[4 - o], 0.0)
        term = shifted(low, CHANS - o) * weight
        total = term if total is None else total + term
        weight = jnp.where(channel + o >= CHANS, kernel_taps[4 + o], 0.0)
        total = total + shifted(high, o - CHANS) * weight
    return total


def body(
    vis, coh, vis_tail, coh_tail, jones, duals,
    jones_out, cons_out, duals_out, norms_out,
    cbuf, vbuf, ct_re, ct_im, v_re, v_im, h_re, h_im, d_re, d_im, mix,
    g, y, part, sent, from_low, from_high, mine, gather_a, gather_b,
    load_sems, vis_sem, send_low, send_high, low_sem, high_sem,
    a_send, a_recv, b_send, b_recv,
    *, entries,
):
    count = lax.axis_size("chan")
    me = lax.axis_index("chan")
    core = lax.rem(me, 2)
    at_z = lax.rem(me // 2, 8)
    at_y = me // 16
    slot_a = at_y * 2 + core
    slot_b = at_z

    def peer_a(i):
        other = lax.rem(slot_a + i, 8)
        return (other // 2) * 16 + at_z * 2 + lax.rem(other, 2)

    def peer_b(i):
        other = lax.rem(slot_b + i, 8)
        return at_y * 16 + other * 2 + core

    loads = [
        pltpu.make_async_copy(
            coh.at[:, :, pl.ds(LANES * j, LANES)], cbuf.at[j], load_sems.at[j])
        for j in range(FULL)
    ]
    vis_load = pltpu.make_async_copy(
        vis.at[:, 0, pl.ds(0, LANES * FULL)], vbuf, vis_sem)
    for copy in loads:
        copy.start()
    vis_load.start()

    @pl.when(me == 0)
    def _():
        from_low[...] = jnp.zeros_like(from_low)

    @pl.when(me == count - 1)
    def _():
        from_high[...] = jnp.zeros_like(from_high)

    barrier = pltpu.get_barrier_semaphore()
    for i in range(1, 8):
        pl.semaphore_signal(barrier, inc=1, device_id=to_chan(peer_a(i)))
        pl.semaphore_signal(barrier, inc=1, device_id=to_chan(peer_b(i)))

    @pl.when(me > 0)
    def _():
        pl.semaphore_signal(barrier, inc=1, device_id=to_chan(me - 1))

    @pl.when(me < count - 1)
    def _():
        pl.semaphore_signal(barrier, inc=1, device_id=to_chan(me + 1))

    lane_row = lax.broadcasted_iota(jnp.int32, (1, LANES), 1)
    channel = lax.rem(lane_row, CHANS)

    g[...] = jnp.zeros_like(g)
    y[...] = jnp.zeros_like(y)
    for source, target in ((jones, g), (duals, y)):
        turned = source[...].T
        target[pl.ds(0, STATIONS), :] = turned[:, :LANES]
        target[pl.ds(SIDE, STATIONS), :] = turned[:, LANES:]

    row = lax.broadcasted_iota(jnp.int32, (2 * LANES, LANES), 0)
    lane = lax.broadcasted_iota(jnp.int32, (2 * LANES, LANES), 1)
    mix[...] = jnp.where((row & 67) == (lane & 67), 1.0, 0.0).astype(BF16)

    turned_rows = cbuf.reshape(FULL, 2 * LANES, LANES)
    is_real = (lane_row & 63) < 4
    is_imag = ((lane_row & 63) >= 4) & ((lane_row & 63) < 8)
    blank = jnp.zeros((56, LANES), F32)

    def put(j, coherent, seen):
        rows = pl.ds(LANES * j, LANES)
        turned = coherent.T
        c_real = turned[:, :LANES].astype(F32)
        c_imag = turned[:, LANES:].astype(F32)
        stacked = jnp.concatenate(
            [seen[0:4], seen[8:12], blank, seen[4:8], seen[12:16], blank], axis=0)
        pairs = stacked.T
        seen_real = jnp.where(is_real, pairs, 0.0)
        seen_imag = jnp.where(is_imag, pairs, 0.0)
        if j == FULL:
            live = lax.broadcasted_iota(jnp.int32, (LANES, LANES), 0) < PAIRS - LANES * FULL
            c_real = jnp.where(live, c_real, 0.0)
            c_imag = jnp.where(live, c_imag, 0.0)
            seen_real = jnp.where(live, seen_real, 0.0)
            seen_imag = jnp.where(live, seen_imag, 0.0)
        ct_re[rows, :] = c_real
        ct_im[rows, :] = c_imag
        v_re[rows, :] = seen_real
        v_im[rows, :] = seen_imag

    put(FULL, coh_tail[...].reshape(2 * LANES, LANES), vis_tail[:, 0, :])
    rest = pl.ds(LANES * TILES, FLAT - LANES * TILES)
    for ref in (ct_re, ct_im, v_re, v_im):
        ref[rest, :] = jnp.zeros((FLAT - LANES * TILES, LANES), F32)
    vis_load.wait()
    for j in range(FULL):
        loads[j].wait()
        put(j, turned_rows[j], vbuf[:, LANES * j:LANES * (j + 1)])
    for p in range(STATIONS):
        ct_re[pl.ds(63 * p, 1), :] = jnp.zeros((1, LANES), F32)
        ct_im[pl.ds(63 * p, 1), :] = jnp.zeros((1, LANES), F32)

    def model(block):
        q_real = g[pl.ds(0, SIDE), :]
        q_imag = g[pl.ds(SIDE, SIDE), :]
        left_real, left_imag = [], []
        for i in range(BLOCK):
            p = block * BLOCK + i
            pairs = pl.ds(STATIONS * p, SIDE)
            spot = pl.ds(pl.multiple_of(SIDE * p, SIDE), SIDE)
            c_real = ct_re[pairs, :]
            c_imag = ct_im[pairs, :]
            half_real = c_real * q_real + c_imag * q_imag
            half_imag = c_imag * q_real - c_real * q_imag
            h_re[spot, :] = half_real
            h_im[spot, :] = half_imag
            p_real = g[pl.ds(p, 1), :]
            p_imag = g[pl.ds(SIDE + p, 1), :]
            m_real = (p_real * half_real - p_imag * half_imag) - v_re[pairs, :]
            m_imag = (p_real * half_imag + p_imag * half_real) - v_im[pairs, :]
            for m, left in ((m_real, left_real), (m_imag, left_imag)):
                high = m.astype(BF16)
                left.append(jnp.concatenate([high, (m - high.astype(F32)).astype(BF16)], axis=1))
        spot = pl.ds(pl.multiple_of(ROWS * block, ROWS), ROWS)
        d_re[spot, :] = jnp.dot(jnp.concatenate(left_real, axis=0), mix[...], preferred_element_type=F32)
        d_im[spot, :] = jnp.dot(jnp.concatenate(left_imag, axis=0), mix[...], preferred_element_type=F32)

    def gather_sums(block):
        for i in range(BLOCK):
            p = block * BLOCK + i
            spot = pl.ds(pl.multiple_of(SIDE * p, SIDE), SIDE)
            a, b = h_re[spot, :], h_im[spot, :]
            u, w = d_re[spot, :], d_im[spot, :]
            into = pl.ds(pl.multiple_of(8 * p, 8), 8)

            def folded(x):
                return jnp.sum(x.reshape(8, 8, LANES), axis=0)

            part[0, into, :] = folded(u * a + w * b)
            part[1, into, :] = folded(w * a - u * b)
            part[2, into, :] = folded(a * a + b * b)

    def sums():
        model(0)

        def step(block, carry):
            gather_sums(block - 1)
            model(block)
            return carry

        lax.fori_loop(1, BLOCKS, step, 0)
        gather_sums(BLOCKS - 1)
        out = []
        for i in range(3):
            tiles = []
            for t in range(8):
                total = part[i, pl.ds(64 * t, 8, stride=8), :]
                for s in range(1, 8):
                    total = total + part[i, pl.ds(64 * t + s, 8, stride=8), :]
                tiles.append(total)
            out.append(jnp.concatenate(tiles, axis=0))
        return jnp.concatenate(out[:2], axis=0), jnp.concatenate([out[2], out[2]], axis=0)

    def exchange(turn):
        to_low = pltpu.make_async_remote_copy(
            sent.at[turn], from_high.at[turn], send_low.at[turn], high_sem.at[turn],
            device_id=to_chan(me - 1))
        to_high = pltpu.make_async_remote_copy(
            sent.at[turn], from_low.at[turn], send_high.at[turn], low_sem.at[turn],
            device_id=to_chan(me + 1))
        return to_low, to_high

    def send(turn):
        to_low, to_high = exchange(turn)

        @pl.when(me > 0)
        def _():
            to_low.start()

        @pl.when(me < count - 1)
        def _():
            to_high.start()

    def receive(turn):
        to_low, to_high = exchange(turn)

        @pl.when(me > 0)
        def _():
            to_low.wait_send()
            to_high.wait_recv()

        @pl.when(me < count - 1)
        def _():
            to_high.wait_send()
            to_low.wait_recv()

    def column_sums(x):
        return jnp.sum(x, axis=0, keepdims=True)

    numer, denom = sums()
    gain0 = g[...]
    dual0 = y[...]
    gain1 = (gain0 * denom - numer + penalty * (gain0 - dual0)) / (denom + penalty)
    summed1 = gain1 + dual0
    sent[0] = summed1
    pl.semaphore_wait(barrier, 14 + (me > 0).astype(jnp.int32) + (me < count - 1).astype(jnp.int32))
    send(0)
    z_own = smooth_own(summed1, channel)
    sent[2] = gain0
    g[...] = gain1
    sent[3] = z_own

    numer, denom = sums()
    receive(0)
    gain1 = g[...]
    fresh1 = sent[3] + smooth_sides(from_low[0], from_high[0], channel)
    dual1 = y[...] + gain1 - fresh1
    gain2 = (gain1 * denom - numer + penalty * (fresh1 - dual1)) / (denom + penalty)
    summed2 = gain2 + dual1
    sent[1] = summed2
    send(1)
    gap = gain1 - fresh1
    moved = fresh1 - sent[2]
    first = [column_sums(gap * gap), column_sums(moved * moved) * (penalty * penalty)]
    z_own = smooth_own(summed2, channel)

    def turned_out(x, ref):
        both = jnp.concatenate([x[:SIDE], x[SIDE:]], axis=1).T
        ref[...] = both[:, :STATIONS]

    turned_out(gain2, jones_out)
    receive(1)
    fresh2 = z_own + smooth_sides(from_low[1], from_high[1], channel)
    gap = gain2 - fresh2
    moved = fresh2 - fresh1
    mine[0] = jnp.concatenate(
        first + [column_sums(gap * gap), column_sums(moved * moved) * (penalty * penalty)], axis=0)

    def spread(source, gathered, slot, peer, send_sems, recv_sem):
        copies = []
        for i in range(1, 8):
            copy = pltpu.make_async_remote_copy(
                source, gathered.at[slot], send_sems.at[i], recv_sem, device_id=to_chan(peer(i)))
            copy.start()
            copies.append(copy)
        gathered[slot] = source[...]
        return copies

    def settle(gathered, copies, recv_sem):
        pltpu.make_async_copy(gathered.at[pl.ds(0, 7)], gathered.at[pl.ds(0, 7)], recv_sem).wait()
        for copy in copies:
            copy.wait_send()
        return jnp.sum(gathered[...], axis=0)

    copies = spread(mine.at[0], gather_a, slot_a, peer_a, a_send, a_recv.at[0])
    turned_out(fresh2, cons_out)
    turned_out(dual1 + gain2 - fresh2, duals_out)
    mine[1] = settle(gather_a, copies, a_recv.at[0])
    copies = spread(mine.at[1], gather_b, slot_b, peer_b, b_send, b_recv.at[0])
    total = settle(gather_b, copies, b_recv.at[0])
    total = jnp.sum(total, axis=1, keepdims=True) / entries
    left = lax.broadcasted_iota(jnp.int32, (1, 2), 1) == 0
    norms_out[...] = jnp.concatenate(
        [jnp.where(left, total[0:1], total[1:2]), jnp.where(left, total[2:3], total[3:4])], axis=0)


def local(visibility, coherency, jones_start, duals_start):
    shape = jones_start.shape
    entries = jones_start.size * lax.axis_size("chan")
    vis = visibility.reshape(16, 1, PAIRS)
    coh = coherency.reshape(64, CHANS, PAIRS)
    jones = jones_start.reshape(256, STATIONS)
    duals = duals_start.reshape(256, STATIONS)
    vmem = pl.BlockSpec(memory_space=pltpu.VMEM)
    hbm = pl.BlockSpec(memory_space=pltpu.HBM)
    gains = jax.ShapeDtypeStruct((256, STATIONS), F32)
    pairs = pltpu.VMEM((FLAT, LANES), F32)
    grid_pairs = pltpu.VMEM((SIDE * SIDE, LANES), F32)
    dma = pltpu.SemaphoreType.DMA
    out = pl.pallas_call(
        functools.partial(body, entries=entries),
        grid=(1,),
        out_shape=[gains, gains, gains, jax.ShapeDtypeStruct((2, 2), F32)],
        in_specs=[
            hbm, hbm,
            pl.BlockSpec((16, 1, LANES), lambda i: (0, 0, FULL)),
            pl.BlockSpec((64, CHANS, LANES), lambda i: (0, 0, FULL)),
            vmem, vmem,
        ],
        out_specs=[vmem] * 4,
        scratch_shapes=[
            pltpu.VMEM((FULL, 64, CHANS, LANES), BF16),
            pltpu.VMEM((16, LANES * FULL), F32),
            pairs, pairs, pairs, pairs,
            grid_pairs, grid_pairs, grid_pairs, grid_pairs,
            pltpu.VMEM((2 * LANES, LANES), BF16),
            pltpu.VMEM((2 * SIDE, LANES), F32),
            pltpu.VMEM((2 * SIDE, LANES), F32),
            pltpu.VMEM((3, 8 * SIDE, LANES), F32),
            pltpu.VMEM((4, 2 * SIDE, LANES), F32),
            pltpu.VMEM((2, 2 * SIDE, LANES), F32),
            pltpu.VMEM((2, 2 * SIDE, LANES), F32),
            pltpu.VMEM((2, 4, LANES), F32),
            pltpu.VMEM((8, 4, LANES), F32),
            pltpu.VMEM((8, 4, LANES), F32),
            dma((FULL,)), dma, dma((2,)), dma((2,)), dma((2,)), dma((2,)),
            dma((8,)), dma((1,)), dma((8,)), dma((1,)),
        ],
        compiler_params=pltpu.CompilerParams(
            vmem_limit_bytes=60 * 2**20, collective_id=0, has_side_effects=True),
    )(vis, coh, vis, coh, jones, duals)
    return tuple(part.reshape(shape) for part in out[:3]) + (out[3],)


def solution(mesh):
    gain = P(None, None, "slot", "chan", None)
    return jax.shard_map(
        local,
        mesh=mesh,
        in_specs=(P(None, None, "chan", "slot", None), P(None, None, None, "chan", "slot", None), gain, gain),
        out_specs=(gain, gain, gain, P("slot", None)),
        check_vma=False,
    )
```

time: 161 us -> 40.5 us (0.25)
  local copies, waits for them, and re-layouts: 85.3 us -> 5.9 us
  other arithmetic: 34.8 us -> 0 us
  Pallas kernels: 0 us -> 33.7 us
  starting transfers between devices: 25.2 us -> 0 us
  waiting for transfers between devices: 12 us -> 0 us
    mul x19 -> x0, local copies, waits for them, and re-layouts: 59.9 us -> none  [the longest x11 31.1 us: jones_update(): half_real = left_real * sky_real - left_imag * sky_imag]
    pallas_call x0 -> x1, Pallas kernels: none -> 33.7 us  [local(): pl.pallas_call(functools.partial(body, entries=entries), grid=(1,), out_s...]
    reduce_sum x6 -> x0, other arithmetic: 27.4 us -> none  [the longest x2 19.9 us: jones_update(): jnp.sum(rest_real * weight_real - rest_imag * weight_imag, axis=(3, 5))]
    convert_element_type x2 -> x0, local copies, waits for them, and re-layouts: 16.6 us -> none  [the longest x1 8.38 us: jones_update(): sky_real = coherency[0].astype(jnp.float32).reshape(grid_shape)]
    all_to_all x1 -> x0, starting transfers between devices: 12.8 us -> none  [sent_to_all(): return lax.all_to_all(copies, axis, split_axis=0, concat_axis=0, tiled=True)]
    ppermute x4 -> x0, starting transfers between devices: 12.4 us -> none  [the longest x2 8.37 us: padded_2(): lax.ppermute(lax.slice_in_dim(block, block.shape[dim] - width, None, axis...]
    all_to_all x1 -> x0, waiting for transfers between devices: 7.62 us -> none  [sent_to_all(): return lax.all_to_all(copies, axis, split_axis=0, concat_axis=0, tiled=True)]
    ppermute x4 -> x0, waiting for transfers between devices: 4.36 us -> none  [the longest x2 4.35 us: padded_2(): lax.ppermute(lax.slice_in_dim(block, 0, width, axis=dim), axis, backward)]
  transfers between devices with their start and end apart: 5 -> 0, of which waited for: 2 -> 0; matrix products, arithmetic and copies ran while one was open for 30% -> 0% of each run, Pallas kernels for 0% -> 0%
where the time goes in v1:
time: 40.5 us; the launch traced here: 40.3 us
  Pallas kernels  33.7 us (83%)
  local copies, waits for them, and re-layouts  5.9 us (15%)
  between operations  0.64 us (2%)
    pallas_call x1, Pallas kernels, local(): pl.pallas_call(functools.partial(body, entries=entries), grid=(1,), out_s...  33.7 us
    unnamed x4, local copies, waits for them, and re-layouts  5.9 us

profile of v1, /device:TPU:1, one launch (start us, length us, event | category | flops | bytes accessed | tf_op | source)
XLA Modules:
  0.0 40.3 jit_solution(5597291243137120719)
XLA Ops:
  0.6 33.7 %shard_map.75 = (f32[256,62]{1,0:T(8,128)}, f32[256,62]{1,0:T(8,128)}, f32[256,62]{1,0:T(8,128)}, f32[2,2]{1,0:T(2,128)}) custom-call(f32[16,1,3844]{2,1,0:T(1,128)} %bitcast.9, bf16[64,4,3844]{2,1,0:T(4,128)(2,1)} %bitcast.7, f32[16,1,3844]{2,1,0:T(1,128)} %bitcast.10, bf16[64,4,3844]{2,1,0:T(4,128)(2,1)} %bitcast.8, f32[256,62]{1,0:T(8,128)} %bitcast.11, ...), custom_call_target="tpu_custom_call" | custom-call | tf_op jit(solution)/shard_map/pallas_call | solution.py:342
  34.4 1.6 %copy.12 = f32[2,2,16,4,62]{4,3,2,1,0:T(4,128)} copy(f32[2,2,16,4,62]{4,3,2,1,0:T(4,128)} %bitcast.15) | data formatting | bytes 126976
  36.0 1.6 %copy.13 = f32[2,2,16,4,62]{4,3,2,1,0:T(4,128)} copy(f32[2,2,16,4,62]{4,3,2,1,0:T(4,128)} %bitcast.14) | data formatting | bytes 126976
  37.5 1.6 %copy.14 = f32[2,2,16,4,62]{4,3,2,1,0:T(4,128)} copy(f32[2,2,16,4,62]{4,3,2,1,0:T(4,128)} %bitcast.13) | data formatting | bytes 126976
  39.1 1.2 %copy.15 = f32[2,2]{1,0:T(2,128)} copy(f32[2,2]{1,0:T(2,128)} %get-tuple-element.19) | data formatting | bytes 32

commit v2 on v1

--- a/solution.py
+++ b/solution.py
@@ -18,6 +18,8 @@
 BLOCK = 4
 BLOCKS = SIDE // BLOCK
 ROWS = BLOCK * SIDE
+GROUP = 8
+VMEM_LIMIT = 65_500_000
 
 penalty = 8.0
 kernel_taps = (0.04, 0.06, 0.1, 0.15, 0.3, 0.15, 0.1, 0.06, 0.04)
@@ -57,36 +59,24 @@
     vis, coh, vis_tail, coh_tail, jones, duals,
     jones_out, cons_out, duals_out, norms_out,
     cbuf, vbuf, ct_re, ct_im, v_re, v_im, h_re, h_im, d_re, d_im, mix,
-    g, y, part, sent, from_low, from_high, mine, gather_a, gather_b,
+    g, y, part, left, sent, from_low, from_high, mine, gathered,
     load_sems, vis_sem, send_low, send_high, low_sem, high_sem,
-    a_send, a_recv, b_send, b_recv,
+    norm_send, norm_recv,
     *, entries,
 ):
     count = lax.axis_size("chan")
     me = lax.axis_index("chan")
-    core = lax.rem(me, 2)
-    at_z = lax.rem(me // 2, 8)
-    at_y = me // 16
-    slot_a = at_y * 2 + core
-    slot_b = at_z
-
-    def peer_a(i):
-        other = lax.rem(slot_a + i, 8)
-        return (other // 2) * 16 + at_z * 2 + lax.rem(other, 2)
-
-    def peer_b(i):
-        other = lax.rem(slot_b + i, 8)
-        return at_y * 16 + other * 2 + core
-
-    loads = [
-        pltpu.make_async_copy(
-            coh.at[:, :, pl.ds(LANES * j, LANES)], cbuf.at[j], load_sems.at[j])
-        for j in range(FULL)
-    ]
+    loads = []
+    for first in range(0, FULL, GROUP):
+        size = min(GROUP, FULL - first)
+        sem = load_sems.at[first // GROUP]
+        for j in range(first, first + size):
+            pltpu.make_async_copy(
+                coh.at[:, :, pl.ds(LANES * j, LANES)], cbuf.at[j], sem).start()
+        span = cbuf.at[pl.ds(first, size)]
+        loads.append((first, size, pltpu.make_async_copy(span, span, sem)))
     vis_load = pltpu.make_async_copy(
         vis.at[:, 0, pl.ds(0, LANES * FULL)], vbuf, vis_sem)
-    for copy in loads:
-        copy.start()
     vis_load.start()
 
     @pl.when(me == 0)
@@ -98,17 +88,10 @@
         from_high[...] = jnp.zeros_like(from_high)
 
     barrier = pltpu.get_barrier_semaphore()
-    for i in range(1, 8):
-        pl.semaphore_signal(barrier, inc=1, device_id=to_chan(peer_a(i)))
-        pl.semaphore_signal(barrier, inc=1, device_id=to_chan(peer_b(i)))
-
-    @pl.when(me > 0)
-    def _():
-        pl.semaphore_signal(barrier, inc=1, device_id=to_chan(me - 1))
-
-    @pl.when(me < count - 1)
-    def _():
-        pl.semaphore_signal(barrier, inc=1, device_id=to_chan(me + 1))
+
+    @pl.loop(1, count)
+    def _(i):
+        pl.semaphore_signal(barrier, inc=1, device_id=to_chan(lax.rem(me + i, count)))
 
     lane_row = lax.broadcasted_iota(jnp.int32, (1, LANES), 1)
     channel = lax.rem(lane_row, CHANS)
@@ -125,39 +108,43 @@
     mix[...] = jnp.where((row & 67) == (lane & 67), 1.0, 0.0).astype(BF16)
 
     turned_rows = cbuf.reshape(FULL, 2 * LANES, LANES)
-    is_real = (lane_row & 63) < 4
-    is_imag = ((lane_row & 63) >= 4) & ((lane_row & 63) < 8)
-    blank = jnp.zeros((56, LANES), F32)
-
-    def put(j, coherent, seen):
+    place = (lane_row & 63) // CHANS
+    vis_load.wait()
+
+    def put(j, coherent, pairs):
         rows = pl.ds(LANES * j, LANES)
         turned = coherent.T
-        c_real = turned[:, :LANES].astype(F32)
-        c_imag = turned[:, LANES:].astype(F32)
-        stacked = jnp.concatenate(
-            [seen[0:4], seen[8:12], blank, seen[4:8], seen[12:16], blank], axis=0)
-        pairs = stacked.T
-        seen_real = jnp.where(is_real, pairs, 0.0)
-        seen_imag = jnp.where(is_imag, pairs, 0.0)
-        if j == FULL:
-            live = lax.broadcasted_iota(jnp.int32, (LANES, LANES), 0) < PAIRS - LANES * FULL
-            c_real = jnp.where(live, c_real, 0.0)
-            c_imag = jnp.where(live, c_imag, 0.0)
-            seen_real = jnp.where(live, seen_real, 0.0)
-            seen_imag = jnp.where(live, seen_imag, 0.0)
-        ct_re[rows, :] = c_real
-        ct_im[rows, :] = c_imag
-        v_re[rows, :] = seen_real
-        v_im[rows, :] = seen_imag
-
-    put(FULL, coh_tail[...].reshape(2 * LANES, LANES), vis_tail[:, 0, :])
+        values = [
+            turned[:, :LANES].astype(F32),
+            turned[:, LANES:].astype(F32),
+            jnp.where(place == 2 * (j % GROUP), pairs, 0.0),
+            jnp.where(place == 2 * (j % GROUP) + 1, pairs, 0.0),
+        ]
+        for ref, value in zip((ct_re, ct_im, v_re, v_im), values):
+            if j == FULL:
+                live = lax.broadcasted_iota(jnp.int32, (LANES, LANES), 0) < PAIRS - LANES * FULL
+                value = jnp.where(live, value, 0.0)
+            ref[rows, :] = value
+
     rest = pl.ds(LANES * TILES, FLAT - LANES * TILES)
     for ref in (ct_re, ct_im, v_re, v_im):
         ref[rest, :] = jnp.zeros((FLAT - LANES * TILES, LANES), F32)
-    vis_load.wait()
-    for j in range(FULL):
-        loads[j].wait()
-        put(j, turned_rows[j], vbuf[:, LANES * j:LANES * (j + 1)])
+    for first, size, load in loads:
+        load.wait()
+        seen = [vbuf[:, LANES * j:LANES * (j + 1)] for j in range(first, first + size)]
+        if first + size == FULL:
+            seen.append(vis_tail[:, 0, :])
+        halves = []
+        for pol in range(2):
+            for each in seen:
+                halves += [each[4 * pol:4 * pol + 4], each[8 + 4 * pol:12 + 4 * pol]]
+            if len(seen) < GROUP:
+                halves.append(jnp.zeros((8 * (GROUP - len(seen)), LANES), F32))
+        pairs = jnp.concatenate(halves, axis=0).T
+        for j in range(first, first + size):
+            put(j, turned_rows[j], pairs)
+        if first + size == FULL:
+            put(FULL, coh_tail[...].reshape(2 * LANES, LANES), pairs)
     for p in range(STATIONS):
         ct_re[pl.ds(63 * p, 1), :] = jnp.zeros((1, LANES), F32)
         ct_im[pl.ds(63 * p, 1), :] = jnp.zeros((1, LANES), F32)
@@ -165,7 +152,6 @@
     def model(block):
         q_real = g[pl.ds(0, SIDE), :]
         q_imag = g[pl.ds(SIDE, SIDE), :]
-        left_real, left_imag = [], []
         for i in range(BLOCK):
             p = block * BLOCK + i
             pairs = pl.ds(STATIONS * p, SIDE)
@@ -180,12 +166,15 @@
             p_imag = g[pl.ds(SIDE + p, 1), :]
             m_real = (p_real * half_real - p_imag * half_imag) - v_re[pairs, :]
             m_imag = (p_real * half_imag + p_imag * half_real) - v_im[pairs, :]
-            for m, left in ((m_real, left_real), (m_imag, left_imag)):
+            for side, m in enumerate((m_real, m_imag)):
                 high = m.astype(BF16)
-                left.append(jnp.concatenate([high, (m - high.astype(F32)).astype(BF16)], axis=1))
+                left[side, spot, :LANES] = high
+                left[side, spot, LANES:] = (m - high.astype(F32)).astype(BF16)
+
+    def lane_sums(block):
         spot = pl.ds(pl.multiple_of(ROWS * block, ROWS), ROWS)
-        d_re[spot, :] = jnp.dot(jnp.concatenate(left_real, axis=0), mix[...], preferred_element_type=F32)
-        d_im[spot, :] = jnp.dot(jnp.concatenate(left_imag, axis=0), mix[...], preferred_element_type=F32)
+        d_re[spot, :] = jnp.dot(left[0, spot, :], mix[...], preferred_element_type=F32)
+        d_im[spot, :] = jnp.dot(left[1, spot, :], mix[...], preferred_element_type=F32)
 
     def gather_sums(block):
         for i in range(BLOCK):
@@ -204,13 +193,18 @@
 
     def sums():
         model(0)
+        lane_sums(0)
+        model(1)
 
         def step(block, carry):
-            gather_sums(block - 1)
+            gather_sums(block - 2)
+            lane_sums(block - 1)
             model(block)
             return carry
 
-        lax.fori_loop(1, BLOCKS, step, 0)
+        lax.fori_loop(2, BLOCKS, step, 0)
+        gather_sums(BLOCKS - 2)
+        lane_sums(BLOCKS - 1)
         gather_sums(BLOCKS - 1)
         out = []
         for i in range(3):
@@ -265,7 +259,7 @@
     gain1 = (gain0 * denom - numer + penalty * (gain0 - dual0)) / (denom + penalty)
     summed1 = gain1 + dual0
     sent[0] = summed1
-    pl.semaphore_wait(barrier, 14 + (me > 0).astype(jnp.int32) + (me < count - 1).astype(jnp.int32))
+    pl.semaphore_wait(barrier, count - 1)
     send(0)
     z_own = smooth_own(summed1, channel)
     sent[2] = gain0
@@ -295,35 +289,44 @@
     fresh2 = z_own + smooth_sides(from_low[1], from_high[1], channel)
     gap = gain2 - fresh2
     moved = fresh2 - fresh1
-    mine[0] = jnp.concatenate(
+    four = jnp.concatenate(
         first + [column_sums(gap * gap), column_sums(moved * moved) * (penalty * penalty)], axis=0)
-
-    def spread(source, gathered, slot, peer, send_sems, recv_sem):
-        copies = []
-        for i in range(1, 8):
-            copy = pltpu.make_async_remote_copy(
-                source, gathered.at[slot], send_sems.at[i], recv_sem, device_id=to_chan(peer(i)))
-            copy.start()
-            copies.append(copy)
-        gathered[slot] = source[...]
-        return copies
-
-    def settle(gathered, copies, recv_sem):
-        pltpu.make_async_copy(gathered.at[pl.ds(0, 7)], gathered.at[pl.ds(0, 7)], recv_sem).wait()
-        for copy in copies:
-            copy.wait_send()
-        return jnp.sum(gathered[...], axis=0)
-
-    copies = spread(mine.at[0], gather_a, slot_a, peer_a, a_send, a_recv.at[0])
+    four = jnp.sum(four, axis=1, keepdims=True)
+    own_lane = lax.broadcasted_iota(jnp.int32, (4, LANES), 0) == lax.broadcasted_iota(
+        jnp.int32, (4, LANES), 1)
+    mine[...] = jnp.sum(jnp.where(own_lane, four, 0.0), axis=0, keepdims=True)
+
+    def to_peer(i):
+        return pltpu.make_async_remote_copy(
+            mine, gathered.at[me], norm_send, norm_recv,
+            device_id=to_chan(lax.rem(me + i, count)))
+
+    @pl.loop(1, count)
+    def _(i):
+        to_peer(i).start()
+
+    gathered[me] = mine[...]
     turned_out(fresh2, cons_out)
     turned_out(dual1 + gain2 - fresh2, duals_out)
-    mine[1] = settle(gather_a, copies, a_recv.at[0])
-    copies = spread(mine.at[1], gather_b, slot_b, peer_b, b_send, b_recv.at[0])
-    total = settle(gather_b, copies, b_recv.at[0])
-    total = jnp.sum(total, axis=1, keepdims=True) / entries
-    left = lax.broadcasted_iota(jnp.int32, (1, 2), 1) == 0
+    others = gathered.at[pl.ds(0, count - 1)]
+    pltpu.make_async_copy(others, others, norm_recv).wait()
+    pltpu.make_async_copy(others, others, norm_send).wait()
+    total = jnp.sum(gathered[...], axis=0) / entries
     norms_out[...] = jnp.concatenate(
-        [jnp.where(left, total[0:1], total[1:2]), jnp.where(left, total[2:3], total[3:4])], axis=0)
+        [total[:, :2], pltpu.roll(total, LANES - 2, axis=1)[:, :2]], axis=0)
+
+
+def write_out(*refs):
+    sems = refs[-1]
+    into = [pltpu.make_async_copy(refs[i], refs[8 + i], sems.at[i]) for i in range(4)]
+    onward = [pltpu.make_async_copy(refs[8 + i], refs[4 + i], sems.at[i]) for i in range(4)]
+    for copy in into:
+        copy.start()
+    for first, second in zip(into, onward):
+        first.wait()
+        second.start()
+    for copy in onward:
+        copy.wait()
 
 
 def local(visibility, coherency, jones_start, duals_start):
@@ -359,18 +362,26 @@
             pltpu.VMEM((2 * SIDE, LANES), F32),
             pltpu.VMEM((2 * SIDE, LANES), F32),
             pltpu.VMEM((3, 8 * SIDE, LANES), F32),
+            pltpu.VMEM((2, SIDE * SIDE, 2 * LANES), BF16),
             pltpu.VMEM((4, 2 * SIDE, LANES), F32),
             pltpu.VMEM((2, 2 * SIDE, LANES), F32),
             pltpu.VMEM((2, 2 * SIDE, LANES), F32),
-            pltpu.VMEM((2, 4, LANES), F32),
-            pltpu.VMEM((8, 4, LANES), F32),
-            pltpu.VMEM((8, 4, LANES), F32),
-            dma((FULL,)), dma, dma((2,)), dma((2,)), dma((2,)), dma((2,)),
-            dma((8,)), dma((1,)), dma((8,)), dma((1,)),
+            pltpu.VMEM((1, LANES), F32),
+            pltpu.VMEM((lax.axis_size("chan"), 1, LANES), F32),
+            dma((-(-FULL // GROUP),)), dma, dma((2,)), dma((2,)), dma((2,)), dma((2,)),
+            dma, dma,
         ],
         compiler_params=pltpu.CompilerParams(
-            vmem_limit_bytes=60 * 2**20, collective_id=0, has_side_effects=True),
+            vmem_limit_bytes=VMEM_LIMIT, collective_id=0, has_side_effects=True),
     )(vis, coh, vis, coh, jones, duals)
+    anywhere = pl.BlockSpec(memory_space=pl.ANY)
+    out = pl.pallas_call(
+        write_out,
+        out_shape=[jax.ShapeDtypeStruct(part.shape, part.dtype) for part in out],
+        in_specs=[anywhere] * 4,
+        out_specs=[anywhere] * 4,
+        scratch_shapes=[pltpu.VMEM(part.shape, part.dtype) for part in out] + [dma((4,))],
+    )(*out)
     return tuple(part.reshape(shape) for part in out[:3]) + (out[3],)
 
 

time: 40.5 us -> 31.6 us (0.78)
  local copies, waits for them, and re-layouts: 5.9 us -> 0 us
  Pallas kernels: 33.7 us -> 30.8 us
    unnamed x4 -> x0, local copies, waits for them, and re-layouts: 5.9 us -> none
    pallas_call x1, Pallas kernels: 33.7 us -> 29.1 us  [local(): pl.pallas_call(functools.partial(body, entries=entries), grid=(1,), out_s...]
    pallas_call x0 -> x1, Pallas kernels: none -> 1.72 us  [local(): pl.pallas_call(write_out, out_shape=[jax.ShapeDtypeStruct(part.shape, par...]
where the time goes in v2:
time: 31.6 us; the launch traced here: 31.4 us
  Pallas kernels  30.8 us (97%)
  between operations  0.64 us (2%)
    pallas_call x1, Pallas kernels, local(): pl.pallas_call(functools.partial(body, entries=entries), grid=(1,), out_s...  29.1 us
    pallas_call x1, Pallas kernels, local(): pl.pallas_call(write_out, out_shape=[jax.ShapeDtypeStruct(part.shape, par...  1.72 us

profile of v2, /device:TPU:1, one launch (start us, length us, event | category | flops | bytes accessed | tf_op | source)
XLA Modules:
  0.0 31.4 jit_solution(2562064080363844477)
XLA Ops:
  0.6 29.1 %shard_map.75 = (f32[256,62]{1,0:T(8,128)}, f32[256,62]{1,0:T(8,128)}, f32[256,62]{1,0:T(8,128)}, f32[2,2]{1,0:T(2,128)}) custom-call(f32[16,1,3844]{2,1,0:T(1,128)} %bitcast.9, bf16[64,4,3844]{2,1,0:T(4,128)(2,1)} %bitcast.7, f32[16,1,3844]{2,1,0:T(1,128)} %bitcast.10, bf16[64,4,3844]{2,1,0:T(4,128)(2,1)} %bitcast.8, f32[256,62]{1,0:T(8,128)} %bitcast.11, ...), custom_call_target="tpu_custom_call" | custom-call | tf_op jit(solution)/shard_map/pallas_call | solution.py:345
  29.7 1.7 %shard_map.76 = (f32[256,62]{1,0:T(8,128)}, f32[256,62]{1,0:T(8,128)}, f32[256,62]{1,0:T(8,128)}, f32[2,2]{1,0:T(2,128)}) custom-call(f32[256,62]{1,0:T(8,128)} %get-tuple-element.12.refs_0_, f32[256,62]{1,0:T(8,128)} %get-tuple-element.13.refs_1_, f32[256,62]{1,0:T(8,128)} %get-tuple-element.14.refs_2_, f32[2,2]{1,0:T(2,128)} %get-tuple-element.15.refs_3_), custom_call_target="tpu_custom_call" | custom-call | tf_op jit(solution)/shard_map/pallas_call | solution.py:378

commit v3 on v2

--- a/solution.py
+++ b/solution.py
@@ -15,10 +15,11 @@
 FULL = PAIRS // LANES
 TILES = FULL + 1
 FLAT = STATIONS * SIDE + 2 * SIDE
-BLOCK = 4
-BLOCKS = SIDE // BLOCK
-ROWS = BLOCK * SIDE
+BLOCK = 31
+BLOCKS = STATIONS // BLOCK
 GROUP = 8
+DOT = 4
+STEP = 16
 VMEM_LIMIT = 65_500_000
 
 penalty = 8.0
@@ -56,10 +57,12 @@
 
 
 def body(
-    vis, coh, vis_tail, coh_tail, jones, duals,
+    vis, coh, jones_in, duals_in,
     jones_out, cons_out, duals_out, norms_out,
-    cbuf, vbuf, ct_re, ct_im, v_re, v_im, h_re, h_im, d_re, d_im, mix,
-    g, y, part, left, sent, from_low, from_high, mine, gathered,
+    gains_buf, norms_buf, out_sems,
+    jones, duals, vis_tail, coh_tail, in_sems,
+    cbuf, vbuf, ct_re, ct_im, v_re, v_im, h_re, h_im, mix,
+    g, y, part, sent, from_low, from_high, mine, gathered,
     load_sems, vis_sem, send_low, send_high, low_sem, high_sem,
     norm_send, norm_recv,
     *, entries,
@@ -78,6 +81,15 @@
     vis_load = pltpu.make_async_copy(
         vis.at[:, 0, pl.ds(0, LANES * FULL)], vbuf, vis_sem)
     vis_load.start()
+    ends = pl.ds(LANES * (FULL - 1), PAIRS - LANES * (FULL - 1))
+    small = [
+        pltpu.make_async_copy(jones_in, jones, in_sems.at[0]),
+        pltpu.make_async_copy(duals_in, duals, in_sems.at[1]),
+        pltpu.make_async_copy(vis.at[:, :, ends], vis_tail, in_sems.at[2]),
+        pltpu.make_async_copy(coh.at[:, :, ends], coh_tail, in_sems.at[3]),
+    ]
+    for copy in small:
+        copy.start()
 
     @pl.when(me == 0)
     def _():
@@ -96,16 +108,18 @@
     lane_row = lax.broadcasted_iota(jnp.int32, (1, LANES), 1)
     channel = lax.rem(lane_row, CHANS)
 
-    g[...] = jnp.zeros_like(g)
-    y[...] = jnp.zeros_like(y)
+    for ref in (g, y, part):
+        ref[...] = jnp.zeros_like(ref)
+    for copy in small:
+        copy.wait()
     for source, target in ((jones, g), (duals, y)):
         turned = source[...].T
         target[pl.ds(0, STATIONS), :] = turned[:, :LANES]
         target[pl.ds(SIDE, STATIONS), :] = turned[:, LANES:]
 
-    row = lax.broadcasted_iota(jnp.int32, (2 * LANES, LANES), 0)
-    lane = lax.broadcasted_iota(jnp.int32, (2 * LANES, LANES), 1)
-    mix[...] = jnp.where((row & 67) == (lane & 67), 1.0, 0.0).astype(BF16)
+    row = lax.broadcasted_iota(jnp.int32, (2 * LANES, 2 * LANES), 0)
+    lane = lax.broadcasted_iota(jnp.int32, (2 * LANES, 2 * LANES), 1)
+    mix[...] = jnp.where((row & 195) == (lane & 195), 1.0, 0.0).astype(BF16)
 
     turned_rows = cbuf.reshape(FULL, 2 * LANES, LANES)
     place = (lane_row & 63) // CHANS
@@ -133,7 +147,8 @@
         load.wait()
         seen = [vbuf[:, LANES * j:LANES * (j + 1)] for j in range(first, first + size)]
         if first + size == FULL:
-            seen.append(vis_tail[:, 0, :])
+            seen.append(jnp.concatenate(
+                [vis_tail[:, 0, LANES:], jnp.zeros((16, 2 * LANES - vis_tail.shape[2]), F32)], axis=1))
         halves = []
         for pol in range(2):
             for each in seen:
@@ -144,68 +159,66 @@
         for j in range(first, first + size):
             put(j, turned_rows[j], pairs)
         if first + size == FULL:
-            put(FULL, coh_tail[...].reshape(2 * LANES, LANES), pairs)
+            put(FULL, jnp.concatenate(
+                [coh_tail[:, :, LANES:], jnp.zeros((64, CHANS, 2 * LANES - coh_tail.shape[2]), BF16)],
+                axis=2).reshape(2 * LANES, LANES), pairs)
     for p in range(STATIONS):
         ct_re[pl.ds(63 * p, 1), :] = jnp.zeros((1, LANES), F32)
         ct_im[pl.ds(63 * p, 1), :] = jnp.zeros((1, LANES), F32)
 
-    def model(block):
-        q_real = g[pl.ds(0, SIDE), :]
-        q_imag = g[pl.ds(SIDE, SIDE), :]
-        for i in range(BLOCK):
-            p = block * BLOCK + i
-            pairs = pl.ds(STATIONS * p, SIDE)
-            spot = pl.ds(pl.multiple_of(SIDE * p, SIDE), SIDE)
+    def model(p):
+        p_real = jnp.broadcast_to(g[pl.ds(p, 1), :], (STEP, LANES))
+        p_imag = jnp.broadcast_to(g[pl.ds(SIDE + p, 1), :], (STEP, LANES))
+        highs, lows = [], []
+        for q in range(0, SIDE, STEP):
+            pairs = pl.ds(STATIONS * p + q, STEP)
+            q_real = g[pl.ds(q, STEP), :]
+            q_imag = g[pl.ds(SIDE + q, STEP), :]
             c_real = ct_re[pairs, :]
             c_imag = ct_im[pairs, :]
             half_real = c_real * q_real + c_imag * q_imag
             half_imag = c_imag * q_real - c_real * q_imag
+            spot = pl.ds(pl.multiple_of(SIDE * p + q, STEP), STEP)
             h_re[spot, :] = half_real
             h_im[spot, :] = half_imag
-            p_real = g[pl.ds(p, 1), :]
-            p_imag = g[pl.ds(SIDE + p, 1), :]
             m_real = (p_real * half_real - p_imag * half_imag) - v_re[pairs, :]
             m_imag = (p_real * half_imag + p_imag * half_real) - v_im[pairs, :]
-            for side, m in enumerate((m_real, m_imag)):
-                high = m.astype(BF16)
-                left[side, spot, :LANES] = high
-                left[side, spot, LANES:] = (m - high.astype(F32)).astype(BF16)
-
-    def lane_sums(block):
-        spot = pl.ds(pl.multiple_of(ROWS * block, ROWS), ROWS)
-        d_re[spot, :] = jnp.dot(left[0, spot, :], mix[...], preferred_element_type=F32)
-        d_im[spot, :] = jnp.dot(left[1, spot, :], mix[...], preferred_element_type=F32)
-
-    def gather_sums(block):
-        for i in range(BLOCK):
-            p = block * BLOCK + i
-            spot = pl.ds(pl.multiple_of(SIDE * p, SIDE), SIDE)
+            m = jnp.concatenate([m_real, m_imag], axis=1)
+            high = m.astype(BF16)
+            highs.append(high)
+            lows.append((m - high.astype(F32)).astype(BF16))
+        return highs, lows
+
+    def gather_sums(p, sums):
+        total = None
+        for q in range(0, SIDE, 8):
+            spot = pl.ds(pl.multiple_of(SIDE * p + q, 8), 8)
             a, b = h_re[spot, :], h_im[spot, :]
-            u, w = d_re[spot, :], d_im[spot, :]
-            into = pl.ds(pl.multiple_of(8 * p, 8), 8)
-
-            def folded(x):
-                return jnp.sum(x.reshape(8, 8, LANES), axis=0)
-
-            part[0, into, :] = folded(u * a + w * b)
-            part[1, into, :] = folded(w * a - u * b)
-            part[2, into, :] = folded(a * a + b * b)
+            u, w = sums[q:q + 8, :LANES], sums[q:q + 8, LANES:]
+            three = (u * a + w * b, w * a - u * b, a * a + b * b)
+            total = three if total is None else [x + y for x, y in zip(total, three)]
+        into = pl.ds(pl.multiple_of(8 * p, 8), 8)
+        for i in range(3):
+            part[i, into, :] = total[i]
 
     def sums():
-        model(0)
-        lane_sums(0)
-        model(1)
-
         def step(block, carry):
-            gather_sums(block - 2)
-            lane_sums(block - 1)
-            model(block)
+            held = []
+            for first in range(0, BLOCK, DOT):
+                size = min(DOT, BLOCK - first)
+                stations = [block * BLOCK + first + i for i in range(size)]
+                models = [model(p) for p in stations]
+                lhs = jnp.concatenate(
+                    [x for side in (0, 1) for each in models for x in each[side]], axis=0)
+                dot = jnp.dot(lhs, mix[...], preferred_element_type=F32)
+                total = dot[:SIDE * size] + dot[SIDE * size:]
+                held.append((stations, total))
+            for stations, total in held:
+                for i, p in enumerate(stations):
+                    gather_sums(p, total[SIDE * i:SIDE * (i + 1)])
             return carry
 
-        lax.fori_loop(2, BLOCKS, step, 0)
-        gather_sums(BLOCKS - 2)
-        lane_sums(BLOCKS - 1)
-        gather_sums(BLOCKS - 1)
+        lax.fori_loop(0, BLOCKS, step, 0)
         out = []
         for i in range(3):
             tiles = []
@@ -280,9 +293,14 @@
     first = [column_sums(gap * gap), column_sums(moved * moved) * (penalty * penalty)]
     z_own = smooth_own(summed2, channel)
 
+    outs = []
+
     def turned_out(x, ref):
         both = jnp.concatenate([x[:SIDE], x[SIDE:]], axis=1).T
-        ref[...] = both[:, :STATIONS]
+        at = len(outs)
+        gains_buf[at] = both[:, :STATIONS]
+        outs.append(pltpu.make_async_copy(gains_buf.at[at], ref, out_sems.at[at]))
+        outs[-1].start()
 
     turned_out(gain2, jones_out)
     receive(1)
@@ -296,14 +314,14 @@
         jnp.int32, (4, LANES), 1)
     mine[...] = jnp.sum(jnp.where(own_lane, four, 0.0), axis=0, keepdims=True)
 
-    def to_peer(i):
-        return pltpu.make_async_remote_copy(
-            mine, gathered.at[me], norm_send, norm_recv,
-            device_id=to_chan(lax.rem(me + i, count)))
-
-    @pl.loop(1, count)
+    @pl.loop(0, count)
     def _(i):
-        to_peer(i).start()
+        peer = lax.rem(i, 8) // 2 * 16 + i // 8 * 2 + lax.rem(i, 2)
+
+        @pl.when(peer != me)
+        def _():
+            pltpu.make_async_remote_copy(
+                mine, gathered.at[me], norm_send, norm_recv, device_id=to_chan(peer)).start()
 
     gathered[me] = mine[...]
     turned_out(fresh2, cons_out)
@@ -312,8 +330,12 @@
     pltpu.make_async_copy(others, others, norm_recv).wait()
     pltpu.make_async_copy(others, others, norm_send).wait()
     total = jnp.sum(gathered[...], axis=0) / entries
-    norms_out[...] = jnp.concatenate(
+    norms_buf[...] = jnp.concatenate(
         [total[:, :2], pltpu.roll(total, LANES - 2, axis=1)[:, :2]], axis=0)
+    outs.append(pltpu.make_async_copy(norms_buf, norms_out, out_sems.at[3]))
+    outs[-1].start()
+    for copy in outs:
+        copy.wait()
 
 
 def write_out(*refs):
@@ -336,7 +358,6 @@
     coh = coherency.reshape(64, CHANS, PAIRS)
     jones = jones_start.reshape(256, STATIONS)
     duals = duals_start.reshape(256, STATIONS)
-    vmem = pl.BlockSpec(memory_space=pltpu.VMEM)
     hbm = pl.BlockSpec(memory_space=pltpu.HBM)
     gains = jax.ShapeDtypeStruct((256, STATIONS), F32)
     pairs = pltpu.VMEM((FLAT, LANES), F32)
@@ -344,25 +365,26 @@
     dma = pltpu.SemaphoreType.DMA
     out = pl.pallas_call(
         functools.partial(body, entries=entries),
-        grid=(1,),
         out_shape=[gains, gains, gains, jax.ShapeDtypeStruct((2, 2), F32)],
-        in_specs=[
-            hbm, hbm,
-            pl.BlockSpec((16, 1, LANES), lambda i: (0, 0, FULL)),
-            pl.BlockSpec((64, CHANS, LANES), lambda i: (0, 0, FULL)),
-            vmem, vmem,
-        ],
-        out_specs=[vmem] * 4,
+        in_specs=[hbm] * 4,
+        out_specs=[hbm] * 4,
         scratch_shapes=[
+            pltpu.VMEM((3, 256, STATIONS), F32),
+            pltpu.VMEM((2, 2), F32),
+            dma((4,)),
+            pltpu.VMEM((256, STATIONS), F32),
+            pltpu.VMEM((256, STATIONS), F32),
+            pltpu.VMEM((16, 1, PAIRS - LANES * (FULL - 1)), F32),
+            pltpu.VMEM((64, CHANS, PAIRS - LANES * (FULL - 1)), BF16),
+            dma((4,)),
             pltpu.VMEM((FULL, 64, CHANS, LANES), BF16),
             pltpu.VMEM((16, LANES * FULL), F32),
             pairs, pairs, pairs, pairs,
-            grid_pairs, grid_pairs, grid_pairs, grid_pairs,
-            pltpu.VMEM((2 * LANES, LANES), BF16),
+            grid_pairs, grid_pairs,
+            pltpu.VMEM((2 * LANES, 2 * LANES), BF16),
             pltpu.VMEM((2 * SIDE, LANES), F32),
             pltpu.VMEM((2 * SIDE, LANES), F32),
             pltpu.VMEM((3, 8 * SIDE, LANES), F32),
-            pltpu.VMEM((2, SIDE * SIDE, 2 * LANES), BF16),
             pltpu.VMEM((4, 2 * SIDE, LANES), F32),
             pltpu.VMEM((2, 2 * SIDE, LANES), F32),
             pltpu.VMEM((2, 2 * SIDE, LANES), F32),
@@ -373,7 +395,7 @@
         ],
         compiler_params=pltpu.CompilerParams(
             vmem_limit_bytes=VMEM_LIMIT, collective_id=0, has_side_effects=True),
-    )(vis, coh, vis, coh, jones, duals)
+    )(vis, coh, jones, duals)
     anywhere = pl.BlockSpec(memory_space=pl.ANY)
     out = pl.pallas_call(
         write_out,

time: 31.6 us -> 28.9 us (0.915)
  Pallas kernels: 30.8 us -> 28.2 us
    pallas_call x1, Pallas kernels: 29.1 us -> 26.4 us  [local(): pl.pallas_call(functools.partial(body, entries=entries), out_shape=[gains...]
where the time goes in v3:
time: 28.9 us; the launch traced here: 28.8 us
  Pallas kernels  28.2 us (98%)
  between operations  0.64 us (2%)
    pallas_call x1, Pallas kernels, local(): pl.pallas_call(functools.partial(body, entries=entries), out_shape=[gains...  26.4 us
    pallas_call x1, Pallas kernels, local(): pl.pallas_call(write_out, out_shape=[jax.ShapeDtypeStruct(part.shape, par...  1.72 us

profile of v3, /device:TPU:1, one launch (start us, length us, event | category | flops | bytes accessed | tf_op | source)
XLA Modules:
  0.0 28.8 jit_solution(12085596731974504707)
XLA Ops:
  0.6 26.4 %shard_map.75 = (f32[256,62]{1,0:T(8,128)}, f32[256,62]{1,0:T(8,128)}, f32[256,62]{1,0:T(8,128)}, f32[2,2]{1,0:T(2,128)}) custom-call(f32[16,1,3844]{2,1,0:T(1,128)} %bitcast.8, bf16[64,4,3844]{2,1,0:T(4,128)(2,1)} %bitcast.7, f32[256,62]{1,0:T(8,128)} %bitcast.9, f32[256,62]{1,0:T(8,128)} %bitcast.10), custom_call_target="tpu_custom_call" | custom-call | tf_op jit(solution)/shard_map/pallas_call | solution.py:366
  27.1 1.7 %shard_map.76 = (f32[256,62]{1,0:T(8,128)}, f32[256,62]{1,0:T(8,128)}, f32[256,62]{1,0:T(8,128)}, f32[2,2]{1,0:T(2,128)}) custom-call(f32[256,62]{1,0:T(8,128)} %get-tuple-element.12.refs_0_, f32[256,62]{1,0:T(8,128)} %get-tuple-element.13.refs_1_, f32[256,62]{1,0:T(8,128)} %get-tuple-element.14.refs_2_, f32[2,2]{1,0:T(2,128)} %get-tuple-element.15.refs_3_), custom_call_target="tpu_custom_call" | custom-call | tf_op jit(solution)/shard_map/pallas_call | solution.py:400

commit v4 on v3

--- a/solution.py
+++ b/solution.py
@@ -15,10 +15,9 @@
 FULL = PAIRS // LANES
 TILES = FULL + 1
 FLAT = STATIONS * SIDE + 2 * SIDE
-BLOCK = 31
-BLOCKS = STATIONS // BLOCK
+HALF = SIDE // 2
 GROUP = 8
-DOT = 4
+DOT = 2
 STEP = 16
 VMEM_LIMIT = 65_500_000
 
@@ -62,13 +61,14 @@
     gains_buf, norms_buf, out_sems,
     jones, duals, vis_tail, coh_tail, in_sems,
     cbuf, vbuf, ct_re, ct_im, v_re, v_im, h_re, h_im, mix,
-    g, y, part, sent, from_low, from_high, mine, gathered,
+    g, y, part, kept, sent, from_low, from_high, mine, gathered,
     load_sems, vis_sem, send_low, send_high, low_sem, high_sem,
     norm_send, norm_recv,
     *, entries,
 ):
     count = lax.axis_size("chan")
     me = lax.axis_index("chan")
+    nought = lax.div(me, 1024)
     loads = []
     for first in range(0, FULL, GROUP):
         size = min(GROUP, FULL - first)
@@ -78,18 +78,19 @@
                 coh.at[:, :, pl.ds(LANES * j, LANES)], cbuf.at[j], sem).start()
         span = cbuf.at[pl.ds(first, size)]
         loads.append((first, size, pltpu.make_async_copy(span, span, sem)))
-    vis_load = pltpu.make_async_copy(
-        vis.at[:, 0, pl.ds(0, LANES * FULL)], vbuf, vis_sem)
-    vis_load.start()
-    ends = pl.ds(LANES * (FULL - 1), PAIRS - LANES * (FULL - 1))
-    small = [
-        pltpu.make_async_copy(jones_in, jones, in_sems.at[0]),
-        pltpu.make_async_copy(duals_in, duals, in_sems.at[1]),
-        pltpu.make_async_copy(vis.at[:, :, ends], vis_tail, in_sems.at[2]),
-        pltpu.make_async_copy(coh.at[:, :, ends], coh_tail, in_sems.at[3]),
-    ]
-    for copy in small:
-        copy.start()
+        if first == 0:
+            vis_load = pltpu.make_async_copy(
+                vis.at[:, 0, pl.ds(0, LANES * FULL)], vbuf, vis_sem)
+            vis_load.start()
+            ends = pl.ds(LANES * (FULL - 1), PAIRS - LANES * (FULL - 1))
+            small = [
+                pltpu.make_async_copy(jones_in, jones, in_sems.at[0]),
+                pltpu.make_async_copy(duals_in, duals, in_sems.at[1]),
+                pltpu.make_async_copy(vis.at[:, :, ends], vis_tail, in_sems.at[2]),
+                pltpu.make_async_copy(coh.at[:, :, ends], coh_tail, in_sems.at[3]),
+            ]
+            for copy in small:
+                copy.start()
 
     @pl.when(me == 0)
     def _():
@@ -101,25 +102,33 @@
 
     barrier = pltpu.get_barrier_semaphore()
 
-    @pl.loop(1, count)
+    @pl.loop(0, 9)
     def _(i):
-        pl.semaphore_signal(barrier, inc=1, device_id=to_chan(lax.rem(me + i, count)))
+        for k in range(7):
+            pl.semaphore_signal(
+                barrier, inc=1, device_id=to_chan(lax.rem(me + 7 * i + k + 1, count)))
 
     lane_row = lax.broadcasted_iota(jnp.int32, (1, LANES), 1)
     channel = lax.rem(lane_row, CHANS)
-
     for ref in (g, y, part):
         ref[...] = jnp.zeros_like(ref)
-    for copy in small:
-        copy.wait()
-    for source, target in ((jones, g), (duals, y)):
-        turned = source[...].T
-        target[pl.ds(0, STATIONS), :] = turned[:, :LANES]
-        target[pl.ds(SIDE, STATIONS), :] = turned[:, LANES:]
 
     row = lax.broadcasted_iota(jnp.int32, (2 * LANES, 2 * LANES), 0)
     lane = lax.broadcasted_iota(jnp.int32, (2 * LANES, 2 * LANES), 1)
     mix[...] = jnp.where((row & 195) == (lane & 195), 1.0, 0.0).astype(BF16)
+    rest = pl.ds(LANES * TILES, FLAT - LANES * TILES)
+    for ref in (ct_re, ct_im, v_re, v_im):
+        ref[rest, :] = jnp.zeros((FLAT - LANES * TILES, LANES), F32)
+
+    for copy in small:
+        copy.wait()
+    for source, target in ((jones, g.at[0]), (duals, y)):
+        turned = source[...].T
+        for part_of, lanes in enumerate((slice(0, LANES), slice(LANES, 2 * LANES))):
+            for half in range(2):
+                size = min(HALF, STATIONS - HALF * half)
+                target[pl.ds(SIDE * half + HALF * part_of, size), :] = (
+                    turned[HALF * half:HALF * half + size, lanes])
 
     turned_rows = cbuf.reshape(FULL, 2 * LANES, LANES)
     place = (lane_row & 63) // CHANS
@@ -140,13 +149,11 @@
                 value = jnp.where(live, value, 0.0)
             ref[rows, :] = value
 
-    rest = pl.ds(LANES * TILES, FLAT - LANES * TILES)
-    for ref in (ct_re, ct_im, v_re, v_im):
-        ref[rest, :] = jnp.zeros((FLAT - LANES * TILES, LANES), F32)
-    for first, size, load in loads:
+    def put_group(first, size, load):
         load.wait()
         seen = [vbuf[:, LANES * j:LANES * (j + 1)] for j in range(first, first + size)]
-        if first + size == FULL:
+        last = first + size == FULL
+        if last:
             seen.append(jnp.concatenate(
                 [vis_tail[:, 0, LANES:], jnp.zeros((16, 2 * LANES - vis_tail.shape[2]), F32)], axis=1))
         halves = []
@@ -158,27 +165,32 @@
         pairs = jnp.concatenate(halves, axis=0).T
         for j in range(first, first + size):
             put(j, turned_rows[j], pairs)
-        if first + size == FULL:
+        if last:
             put(FULL, jnp.concatenate(
                 [coh_tail[:, :, LANES:], jnp.zeros((64, CHANS, 2 * LANES - coh_tail.shape[2]), BF16)],
                 axis=2).reshape(2 * LANES, LANES), pairs)
-    for p in range(STATIONS):
-        ct_re[pl.ds(63 * p, 1), :] = jnp.zeros((1, LANES), F32)
-        ct_im[pl.ds(63 * p, 1), :] = jnp.zeros((1, LANES), F32)
-
-    def model(p):
-        p_real = jnp.broadcast_to(g[pl.ds(p, 1), :], (STEP, LANES))
-        p_imag = jnp.broadcast_to(g[pl.ds(SIDE + p, 1), :], (STEP, LANES))
+        end = PAIRS if last else LANES * (first + size)
+        for p in range(STATIONS):
+            if LANES * first <= (STATIONS + 1) * p < end:
+                for ref in (ct_re, ct_im):
+                    ref[pl.ds((STATIONS + 1) * p, 1), :] = jnp.zeros((1, LANES), F32)
+
+    def gain_row(p):
+        return SIDE * (p // HALF) + p % HALF
+
+    def model(p, gains):
+        p_real = jnp.broadcast_to(gains[pl.ds(gain_row(p), 1), :], (STEP, LANES))
+        p_imag = jnp.broadcast_to(gains[pl.ds(gain_row(p) + HALF, 1), :], (STEP, LANES))
         highs, lows = [], []
         for q in range(0, SIDE, STEP):
-            pairs = pl.ds(STATIONS * p + q, STEP)
-            q_real = g[pl.ds(q, STEP), :]
-            q_imag = g[pl.ds(SIDE + q, STEP), :]
+            pairs = pl.ds(nought + STATIONS * p + q, STEP)
+            q_real = gains[pl.ds(gain_row(q), STEP), :]
+            q_imag = gains[pl.ds(gain_row(q) + HALF, STEP), :]
             c_real = ct_re[pairs, :]
             c_imag = ct_im[pairs, :]
             half_real = c_real * q_real + c_imag * q_imag
             half_imag = c_imag * q_real - c_real * q_imag
-            spot = pl.ds(pl.multiple_of(SIDE * p + q, STEP), STEP)
+            spot = pl.ds(SIDE * p + q, STEP)
             h_re[spot, :] = half_real
             h_im[spot, :] = half_imag
             m_real = (p_real * half_real - p_imag * half_imag) - v_re[pairs, :]
@@ -192,37 +204,33 @@
     def gather_sums(p, sums):
         total = None
         for q in range(0, SIDE, 8):
-            spot = pl.ds(pl.multiple_of(SIDE * p + q, 8), 8)
+            spot = pl.ds(SIDE * p + q, 8)
             a, b = h_re[spot, :], h_im[spot, :]
             u, w = sums[q:q + 8, :LANES], sums[q:q + 8, LANES:]
             three = (u * a + w * b, w * a - u * b, a * a + b * b)
             total = three if total is None else [x + y for x, y in zip(total, three)]
-        into = pl.ds(pl.multiple_of(8 * p, 8), 8)
         for i in range(3):
-            part[i, into, :] = total[i]
-
-    def sums():
-        def step(block, carry):
-            held = []
-            for first in range(0, BLOCK, DOT):
-                size = min(DOT, BLOCK - first)
-                stations = [block * BLOCK + first + i for i in range(size)]
-                models = [model(p) for p in stations]
-                lhs = jnp.concatenate(
-                    [x for side in (0, 1) for each in models for x in each[side]], axis=0)
-                dot = jnp.dot(lhs, mix[...], preferred_element_type=F32)
-                total = dot[:SIDE * size] + dot[SIDE * size:]
-                held.append((stations, total))
-            for stations, total in held:
-                for i, p in enumerate(stations):
-                    gather_sums(p, total[SIDE * i:SIDE * (i + 1)])
-            return carry
-
-        lax.fori_loop(0, BLOCKS, step, 0)
+            part[i, pl.ds(8 * p, 8), :] = total[i]
+
+    def pass_over(first, end, gains):
+        held = []
+        for at in range(first, end, DOT):
+            stations = range(at, min(at + DOT, end))
+            models = [model(p, gains) for p in stations]
+            lhs = jnp.concatenate(
+                [x for side in (0, 1) for each in models for x in each[side]], axis=0)
+            dot = jnp.dot(lhs, mix[...], preferred_element_type=F32)
+            size = SIDE * len(stations)
+            held.append((stations, dot[:size] + dot[size:]))
+        for stations, total in held:
+            for i, p in enumerate(stations):
+                gather_sums(p, total[SIDE * i:SIDE * (i + 1)])
+
+    def sums_of(half):
         out = []
         for i in range(3):
             tiles = []
-            for t in range(8):
+            for t in range(4 * half, 4 * half + 4):
                 total = part[i, pl.ds(64 * t, 8, stride=8), :]
                 for s in range(1, 8):
                     total = total + part[i, pl.ds(64 * t + s, 8, stride=8), :]
@@ -230,17 +238,19 @@
             out.append(jnp.concatenate(tiles, axis=0))
         return jnp.concatenate(out[:2], axis=0), jnp.concatenate([out[2], out[2]], axis=0)
 
-    def exchange(turn):
+    def exchange(turn, half):
+        rows = pl.ds(SIDE * half, SIDE)
+        at = 2 * turn + half
         to_low = pltpu.make_async_remote_copy(
-            sent.at[turn], from_high.at[turn], send_low.at[turn], high_sem.at[turn],
+            sent.at[turn, rows], from_high.at[turn, rows], send_low.at[at], high_sem.at[at],
             device_id=to_chan(me - 1))
         to_high = pltpu.make_async_remote_copy(
-            sent.at[turn], from_low.at[turn], send_high.at[turn], low_sem.at[turn],
+            sent.at[turn, rows], from_low.at[turn, rows], send_high.at[at], low_sem.at[at],
             device_id=to_chan(me + 1))
         return to_low, to_high
 
-    def send(turn):
-        to_low, to_high = exchange(turn)
+    def send(turn, half):
+        to_low, to_high = exchange(turn, half)
 
         @pl.when(me > 0)
         def _():
@@ -250,8 +260,8 @@
         def _():
             to_high.start()
 
-    def receive(turn):
-        to_low, to_high = exchange(turn)
+    def receive(turn, half):
+        to_low, to_high = exchange(turn, half)
 
         @pl.when(me > 0)
         def _():
@@ -266,66 +276,94 @@
     def column_sums(x):
         return jnp.sum(x, axis=0, keepdims=True)
 
-    numer, denom = sums()
-    gain0 = g[...]
-    dual0 = y[...]
-    gain1 = (gain0 * denom - numer + penalty * (gain0 - dual0)) / (denom + penalty)
-    summed1 = gain1 + dual0
-    sent[0] = summed1
-    pl.semaphore_wait(barrier, count - 1)
-    send(0)
-    z_own = smooth_own(summed1, channel)
-    sent[2] = gain0
-    g[...] = gain1
-    sent[3] = z_own
-
-    numer, denom = sums()
-    receive(0)
-    gain1 = g[...]
-    fresh1 = sent[3] + smooth_sides(from_low[0], from_high[0], channel)
-    dual1 = y[...] + gain1 - fresh1
-    gain2 = (gain1 * denom - numer + penalty * (fresh1 - dual1)) / (denom + penalty)
-    summed2 = gain2 + dual1
-    sent[1] = summed2
-    send(1)
-    gap = gain1 - fresh1
-    moved = fresh1 - sent[2]
-    first = [column_sums(gap * gap), column_sums(moved * moved) * (penalty * penalty)]
-    z_own = smooth_own(summed2, channel)
+    def residuals(gap, moved, before):
+        now = [column_sums(gap * gap), column_sums(moved * moved) * (penalty * penalty)]
+        return now if before is None else [x + y for x, y in zip(before, now)]
+
+    def rows_of(half):
+        return pl.ds(SIDE * half, SIDE)
+
+    def first_update(half):
+        rows = rows_of(half)
+        numer, denom = sums_of(half)
+        gain0 = g[0, rows, :]
+        dual0 = y[rows, :]
+        gain1 = (gain0 * denom - numer + penalty * (gain0 - dual0)) / (denom + penalty)
+        summed = gain1 + dual0
+        g[1, rows, :] = gain1
+        sent[0, rows, :] = summed
+        if half == 0:
+            pl.semaphore_wait(barrier, count - 1)
+        send(0, half)
+        kept[0, rows, :] = smooth_own(summed, channel)
+
+    for half in range(2):
+        for load in loads[2 * half:2 * half + 2]:
+            put_group(*load)
+        pass_over(HALF * half, min(HALF * half + HALF, STATIONS), g.at[0])
+        first_update(half)
+
+    first = None
+    for half in range(2):
+        rows = rows_of(half)
+        pass_over(HALF * half, min(HALF * half + HALF, STATIONS), g.at[1])
+        numer, denom = sums_of(half)
+        receive(0, half)
+        gain1 = g[1, rows, :]
+        fresh1 = kept[0, rows, :] + smooth_sides(
+            from_low[0, rows, :], from_high[0, rows, :], channel)
+        dual1 = y[rows, :] + gain1 - fresh1
+        gain2 = (gain1 * denom - numer + penalty * (fresh1 - dual1)) / (denom + penalty)
+        summed = gain2 + dual1
+        sent[1, rows, :] = summed
+        send(1, half)
+        first = residuals(gain1 - fresh1, fresh1 - g[0, rows, :], first)
+        kept[1, rows, :] = smooth_own(summed, channel)
+        kept[2, rows, :] = gain2
+        kept[3, rows, :] = fresh1
+        kept[4, rows, :] = dual1
 
     outs = []
 
     def turned_out(x, ref):
-        both = jnp.concatenate([x[:SIDE], x[SIDE:]], axis=1).T
+        both = jnp.concatenate(
+            [jnp.concatenate([x[:HALF], x[SIDE:SIDE + HALF]], axis=0),
+             jnp.concatenate([x[HALF:SIDE], x[SIDE + HALF:]], axis=0)], axis=1).T
         at = len(outs)
         gains_buf[at] = both[:, :STATIONS]
         outs.append(pltpu.make_async_copy(gains_buf.at[at], ref, out_sems.at[at]))
         outs[-1].start()
 
-    turned_out(gain2, jones_out)
-    receive(1)
-    fresh2 = z_own + smooth_sides(from_low[1], from_high[1], channel)
-    gap = gain2 - fresh2
-    moved = fresh2 - fresh1
-    four = jnp.concatenate(
-        first + [column_sums(gap * gap), column_sums(moved * moved) * (penalty * penalty)], axis=0)
-    four = jnp.sum(four, axis=1, keepdims=True)
+    turned_out(kept[2], jones_out)
+    second = None
+    for half in range(2):
+        rows = rows_of(half)
+        receive(1, half)
+        fresh2 = kept[1, rows, :] + smooth_sides(
+            from_low[1, rows, :], from_high[1, rows, :], channel)
+        gap = kept[2, rows, :] - fresh2
+        second = residuals(gap, fresh2 - kept[3, rows, :], second)
+        kept[0, rows, :] = fresh2
+        kept[4, rows, :] = kept[4, rows, :] + gap
+    four = jnp.sum(jnp.concatenate(first + second, axis=0), axis=1, keepdims=True)
     own_lane = lax.broadcasted_iota(jnp.int32, (4, LANES), 0) == lax.broadcasted_iota(
         jnp.int32, (4, LANES), 1)
     mine[...] = jnp.sum(jnp.where(own_lane, four, 0.0), axis=0, keepdims=True)
 
-    @pl.loop(0, count)
+    rank = lax.rem(me // 2, 8) * 8 + me // 16 * 2 + lax.rem(me, 2)
+
+    @pl.loop(0, 9)
     def _(i):
-        peer = lax.rem(i, 8) // 2 * 16 + i // 8 * 2 + lax.rem(i, 2)
-
-        @pl.when(peer != me)
-        def _():
+        for k in range(7):
+            other = 7 * i + k
+            other = other + (other >= rank).astype(jnp.int32)
+            peer = lax.rem(other, 8) // 2 * 16 + other // 8 * 2 + lax.rem(other, 2)
             pltpu.make_async_remote_copy(
                 mine, gathered.at[me], norm_send, norm_recv, device_id=to_chan(peer)).start()
 
     gathered[me] = mine[...]
-    turned_out(fresh2, cons_out)
-    turned_out(dual1 + gain2 - fresh2, duals_out)
+    turned_out(kept[0], cons_out)
+    turned_out(kept[4], duals_out)
     others = gathered.at[pl.ds(0, count - 1)]
     pltpu.make_async_copy(others, others, norm_recv).wait()
     pltpu.make_async_copy(others, others, norm_send).wait()
@@ -382,15 +420,16 @@
             pairs, pairs, pairs, pairs,
             grid_pairs, grid_pairs,
             pltpu.VMEM((2 * LANES, 2 * LANES), BF16),
-            pltpu.VMEM((2 * SIDE, LANES), F32),
+            pltpu.VMEM((2, 2 * SIDE, LANES), F32),
             pltpu.VMEM((2 * SIDE, LANES), F32),
             pltpu.VMEM((3, 8 * SIDE, LANES), F32),
-            pltpu.VMEM((4, 2 * SIDE, LANES), F32),
+            pltpu.VMEM((5, 2 * SIDE, LANES), F32),
+            pltpu.VMEM((2, 2 * SIDE, LANES), F32),
             pltpu.VMEM((2, 2 * SIDE, LANES), F32),
             pltpu.VMEM((2, 2 * SIDE, LANES), F32),
             pltpu.VMEM((1, LANES), F32),
             pltpu.VMEM((lax.axis_size("chan"), 1, LANES), F32),
-            dma((-(-FULL // GROUP),)), dma, dma((2,)), dma((2,)), dma((2,)), dma((2,)),
+            dma((-(-FULL // GROUP),)), dma, dma((4,)), dma((4,)), dma((4,)), dma((4,)),
             dma, dma,
         ],
         compiler_params=pltpu.CompilerParams(

time: 28.9 us -> 28.2 us (0.976)
  Pallas kernels: 28.2 us -> 27.4 us
    pallas_call x1, Pallas kernels: 26.4 us -> 25.7 us  [local(): pl.pallas_call(functools.partial(body, entries=entries), out_shape=[gains...]
where the time goes in v4:
time: 28.2 us; the launch traced here: 28.1 us
  Pallas kernels  27.4 us (97%)
  between operations  0.64 us (2%)
    pallas_call x1, Pallas kernels, local(): pl.pallas_call(functools.partial(body, entries=entries), out_shape=[gains...  25.7 us
    pallas_call x1, Pallas kernels, local(): pl.pallas_call(write_out, out_shape=[jax.ShapeDtypeStruct(part.shape, par...  1.72 us

profile of v4, /device:TPU:1, one launch (start us, length us, event | category | flops | bytes accessed | tf_op | source)
XLA Modules:
  0.0 28.1 jit_solution(17922072046263330263)
XLA Ops:
  0.6 25.7 %shard_map.75 = (f32[256,62]{1,0:T(8,128)}, f32[256,62]{1,0:T(8,128)}, f32[256,62]{1,0:T(8,128)}, f32[2,2]{1,0:T(2,128)}) custom-call(f32[16,1,3844]{2,1,0:T(1,128)} %bitcast.8, bf16[64,4,3844]{2,1,0:T(4,128)(2,1)} %bitcast.7, f32[256,62]{1,0:T(8,128)} %bitcast.9, f32[256,62]{1,0:T(8,128)} %bitcast.10), custom_call_target="tpu_custom_call" | custom-call | tf_op jit(solution)/shard_map/pallas_call | solution.py:404
  26.3 1.7 %shard_map.76 = (f32[256,62]{1,0:T(8,128)}, f32[256,62]{1,0:T(8,128)}, f32[256,62]{1,0:T(8,128)}, f32[2,2]{1,0:T(2,128)}) custom-call(f32[256,62]{1,0:T(8,128)} %get-tuple-element.12.refs_0_, f32[256,62]{1,0:T(8,128)} %get-tuple-element.13.refs_1_, f32[256,62]{1,0:T(8,128)} %get-tuple-element.14.refs_2_, f32[2,2]{1,0:T(2,128)} %get-tuple-element.15.refs_3_), custom_call_target="tpu_custom_call" | custom-call | tf_op jit(solution)/shard_map/pallas_call | solution.py:439

commit v5 on v4

--- a/solution.py
+++ b/solution.py
@@ -346,9 +346,10 @@
         kept[0, rows, :] = fresh2
         kept[4, rows, :] = kept[4, rows, :] + gap
     four = jnp.sum(jnp.concatenate(first + second, axis=0), axis=1, keepdims=True)
-    own_lane = lax.broadcasted_iota(jnp.int32, (4, LANES), 0) == lax.broadcasted_iota(
-        jnp.int32, (4, LANES), 1)
-    mine[...] = jnp.sum(jnp.where(own_lane, four, 0.0), axis=0, keepdims=True)
+    mine[...] = jnp.where(
+        lane_row == 0,
+        jnp.concatenate([four[0:1], four[2:3]], axis=0),
+        jnp.concatenate([four[1:2], four[3:4]], axis=0))
 
     rank = lax.rem(me // 2, 8) * 8 + me // 16 * 2 + lax.rem(me, 2)
 
@@ -366,12 +367,11 @@
     turned_out(kept[4], duals_out)
     others = gathered.at[pl.ds(0, count - 1)]
     pltpu.make_async_copy(others, others, norm_recv).wait()
-    pltpu.make_async_copy(others, others, norm_send).wait()
     total = jnp.sum(gathered[...], axis=0) / entries
-    norms_buf[...] = jnp.concatenate(
-        [total[:, :2], pltpu.roll(total, LANES - 2, axis=1)[:, :2]], axis=0)
+    norms_buf[...] = total[:, :2]
     outs.append(pltpu.make_async_copy(norms_buf, norms_out, out_sems.at[3]))
     outs[-1].start()
+    pltpu.make_async_copy(others, others, norm_send).wait()
     for copy in outs:
         copy.wait()
 
@@ -427,8 +427,8 @@
             pltpu.VMEM((2, 2 * SIDE, LANES), F32),
             pltpu.VMEM((2, 2 * SIDE, LANES), F32),
             pltpu.VMEM((2, 2 * SIDE, LANES), F32),
-            pltpu.VMEM((1, LANES), F32),
-            pltpu.VMEM((lax.axis_size("chan"), 1, LANES), F32),
+            pltpu.VMEM((2, LANES), F32),
+            pltpu.VMEM((lax.axis_size("chan"), 2, LANES), F32),
             dma((-(-FULL // GROUP),)), dma, dma((4,)), dma((4,)), dma((4,)), dma((4,)),
             dma, dma,
         ],

time: 28.2 us -> 28.5 us (1.011)
  Pallas kernels: 27.4 us -> 27.7 us
    pallas_call x1, Pallas kernels: 25.7 us -> 26 us  [local(): pl.pallas_call(functools.partial(body, entries=entries), out_shape=[gains...]
where the time goes in v5:
time: 28.5 us; the launch traced here: 28.4 us
  Pallas kernels  27.7 us (97%)
  between operations  0.64 us (2%)
    pallas_call x1, Pallas kernels, local(): pl.pallas_call(functools.partial(body, entries=entries), out_shape=[gains...  26 us
    pallas_call x1, Pallas kernels, local(): pl.pallas_call(write_out, out_shape=[jax.ShapeDtypeStruct(part.shape, par...  1.72 us

profile of v5, /device:TPU:1, one launch (start us, length us, event | category | flops | bytes accessed | tf_op | source)
XLA Modules:
  0.0 28.4 jit_solution(17555593461791671225)
XLA Ops:
  0.6 26.0 %shard_map.75 = (f32[256,62]{1,0:T(8,128)}, f32[256,62]{1,0:T(8,128)}, f32[256,62]{1,0:T(8,128)}, f32[2,2]{1,0:T(2,128)}) custom-call(f32[16,1,3844]{2,1,0:T(1,128)} %bitcast.8, bf16[64,4,3844]{2,1,0:T(4,128)(2,1)} %bitcast.7, f32[256,62]{1,0:T(8,128)} %bitcast.9, f32[256,62]{1,0:T(8,128)} %bitcast.10), custom_call_target="tpu_custom_call" | custom-call | tf_op jit(solution)/shard_map/pallas_call | solution.py:404
  26.6 1.7 %shard_map.76 = (f32[256,62]{1,0:T(8,128)}, f32[256,62]{1,0:T(8,128)}, f32[256,62]{1,0:T(8,128)}, f32[2,2]{1,0:T(2,128)}) custom-call(f32[256,62]{1,0:T(8,128)} %get-tuple-element.12.refs_0_, f32[256,62]{1,0:T(8,128)} %get-tuple-element.13.refs_1_, f32[256,62]{1,0:T(8,128)} %get-tuple-element.14.refs_2_, f32[2,2]{1,0:T(2,128)} %get-tuple-element.15.refs_3_), custom_call_target="tpu_custom_call" | custom-call | tf_op jit(solution)/shard_map/pallas_call | solution.py:439
